TPU v7x, 8 devices: a whole 2x2x1 slice. The times are simulated.
8 devices in a mesh: data: 8 (over z, y, x, core).
Axes of the slice: x: 2, y: 2, z: 1, core: 2. Of those that a mesh axis runs over, the one named last changes fastest.
Arguments:
- tokens: bfloat16 [16384, 1280], P('data')
- targets: bfloat16 [16384, 1280], P('data')
- w_in: bfloat16 [4, 1280, 5120], replicated
- w_out: bfloat16 [4, 5120, 1280], replicated
Outputs:
- output 1: float32 [4, 1280, 5120], replicated
- output 2: float32 [4, 5120, 1280], replicated
All inputs are finite; a program needn't handle non-finite values.
Results may differ from a plain program's by a relative error of at most 0.0072231.
Values are sent between devices in bfloat16 or wider.
A program may use at most 1.25 GiB of HBM per device.

v0:
```python
import math
import jax
import jax.numpy as jnp
from jax import lax
from jax.sharding import PartitionSpec as P

CONTRACT_ROWS = (((0,), (0,)), ((), ()))
CONTRACT_LAST = (((1,), (1,)), ((), ()))


def gelu_fn(value):
    return jax.nn.gelu(value, approximate=True)


def solution(mesh):
    group = mesh.shape["data"]

    def local_step(tokens, targets, w_in, w_out):
        local_rows = tokens.shape[0]
        layers = w_in.shape[0]
        half_rows = local_rows // 2
        scale = 1.0 / math.sqrt(local_rows * group)
        grads_in = [None] * layers
        grads_out = [None] * layers
        for micro in range(2):
            hidden = tokens[micro * half_rows:(micro + 1) * half_rows]
            target_mb = targets[micro * half_rows:(micro + 1) * half_rows]
            saved = []
            for layer in range(layers):
                pre_act = jnp.dot(hidden, w_in[layer], preferred_element_type=jnp.float32).astype(jnp.bfloat16)
                gelu_out = gelu_fn(pre_act.astype(jnp.float32)).astype(jnp.bfloat16)
                branch = jnp.dot(gelu_out, w_out[layer], preferred_element_type=jnp.float32)
                saved.append((hidden, pre_act, gelu_out))
                hidden = (hidden.astype(jnp.float32) + branch).astype(jnp.bfloat16)
            cotangent = ((hidden.astype(jnp.float32) - target_mb.astype(jnp.float32)) * scale).astype(jnp.bfloat16)
            for layer in reversed(range(layers)):
                layer_in, pre_act, gelu_out = saved[layer]
                g_out = lax.dot_general(gelu_out, cotangent, CONTRACT_ROWS, preferred_element_type=jnp.float32)
                d_act = lax.dot_general(cotangent, w_out[layer], CONTRACT_LAST, preferred_element_type=jnp.float32)
                _, gelu_vjp = jax.vjp(gelu_fn, pre_act.astype(jnp.float32))
                d_pre = gelu_vjp(d_act)[0].astype(jnp.bfloat16)
                g_in = lax.dot_general(layer_in, d_pre, CONTRACT_ROWS, preferred_element_type=jnp.float32)
                if layer > 0:
                    back_prod = lax.dot_general(d_pre, w_in[layer], CONTRACT_LAST, preferred_element_type=jnp.float32)
                    cotangent = (cotangent.astype(jnp.float32) + back_prod).astype(jnp.bfloat16)
                if micro == 0:
                    grads_in[layer] = g_in
                    grads_out[layer] = g_out
                else:
                    grads_in[layer] = lax.psum(grads_in[layer] + g_in, "data")
                    grads_out[layer] = lax.psum(grads_out[layer] + g_out, "data")
        return jnp.stack(grads_in), jnp.stack(grads_out)

    return jax.shard_map(local_step, mesh=mesh, in_specs=(P("data"), P("data"), P(), P()), out_specs=(P(), P()), check_vma=False)
```

profile of v0, /device:TPU:1, one launch (start us, length us, event | category | flops | bytes accessed | tf_op | source)
XLA Modules:
  0.0 3322.8 jit_solution(8275801459578648095)
XLA Ops:
  48.5 26.1 add_convert_fusion.13
  96.2 24.7 add_convert_fusion.12
  143.2 24.8 add_convert_fusion.11
  190.7 26.3 multiply_convert_fusion.1
  217.0 29.5 fusion.22
  266.6 29.7 fusion.25
  316.5 29.7 fusion.28
  389.3 22.6 fusion.294
  434.5 25.9 add_convert_fusion.6
  482.0 25.0 add_convert_fusion.5
  529.3 24.7 add_convert_fusion.4
  575.5 26.5 multiply_convert_fusion
  602.0 31.2 fusion.10
  653.3 29.8 fusion.13
  703.3 29.8 fusion.16
  754.3 29.8 add_bitcast_fusion.6
  784.1 29.7 add_bitcast_fusion.5
  813.8 29.5 add_bitcast_fusion.4
  843.3 43.0 %fusion.153 = f32[5120,1280]{1,0:T(8,128)} fusion(bf16[1024,5120]{1,0:T(8,128)(2,1)} %fusion.159, bf16[1024,1280]{1,0:T(8,128)(2,1)} %add_convert_fusion.7, bf16[4,5120,1280]{2,1,0:T(8,128)(2,1)} %param.7, bf16[2048,1280]{1,0:T(8,128)(2,1)} %param.4), kind=kOutput, calls=%fused_computation.198 | convolution fusion | flops 26953646080 | bytes 55050240 | tf_op jit(solution)/shard_map/dot_general | solution.py:42
  886.4 44.9 %add_bitcast_fusion.7 = f32[1,1280,5120]{1,2,0:T(8,128)} fusion(f32[5120,1280]{1,0:T(8,128)} %fusion.153, bf16[1024,5120]{1,0:T(8,128)(2,1)} %fusion.162, bf16[1024,1280]{1,0:T(8,128)(2,1)S(1)} %copy-done.8, bf16[4,5120,1280]{2,1,0:T(8,128)(2,1)} %param.7, bf16[2048,1280]{1,0:T(8,128)(2,1)} %param.4), kind=kOutput, calls=%fused_computation.57 | convolution fusion | flops 26960199680 | bytes 81264640 | tf_op jit(solution)/shard_map/dot_general | solution.py:42
  931.4 26.6 fusion.287
  957.9 25.4 fusion.284
  983.3 26.2 fusion.281
  1031.9 29.2 add_bitcast_fusion.2
  1061.1 29.8 add_bitcast_fusion.1
  1090.9 28.6 add_bitcast_fusion
  1119.5 29.3 add_bitcast_fusion.3
  1148.8 939.3 %all-reduce.5.cloned.1.call-done = (f32[1,1280,5120]{1,2,0:T(8,128)}, f32[1,1280,5120]{1,2,0:T(8,128)}, f32[1,1280,5120]{1,2,0:T(8,128)}, f32[1,1280,5120]{1,2,0:T(8,128)}) async-done(((f32[1,1280,5120]{1,2,0:T(8,128)}, f32[1,1280,5120]{1,2,0:T(8,128)}, f32[1,1280,5120]{1,2,0:T(8,128)}, f32[1,1280,5120]{1,2,0:T(8,128)}), (f32[1,1280,5120]{1,2,0:T(8,128)}, f32[1,1280,5120]{1,2,0:T(8,128)}, ...) | async-done | bytes 104857616 | tf_op jit(solution)/shard_map/psum | solution.py:50
  2088.1 69.0 %pad_maximum_fusion = f32[4,1280,5120]{1,2,0:T(8,128)} fusion(f32[1,1280,5120]{1,2,0:T(8,128)} %get-tuple-element.4, f32[1,1280,5120]{1,2,0:T(8,128)} %get-tuple-element.5, f32[1,1280,5120]{1,2,0:T(8,128)} %get-tuple-element.6, f32[1,1280,5120]{1,2,0:T(8,128)} %get-tuple-element.7), kind=kLoop, calls=%fused_computation | loop fusion | flops 78643200 | bytes 209715200 | tf_op jit(solution)/shard_map/stack | solution.py:52
  2157.1 97.1 %copy.12 = f32[4,1280,5120]{2,1,0:T(8,128)} copy(f32[4,1280,5120]{1,2,0:T(8,128)} %pad_maximum_fusion) | data formatting | bytes 209715200
  2254.2 992.5 %all-reduce.7.cloned.1.call-done = (f32[1,5120,1280]{2,1,0:T(8,128)}, f32[1,5120,1280]{2,1,0:T(8,128)}, f32[1,5120,1280]{2,1,0:T(8,128)}, f32[1,5120,1280]{2,1,0:T(8,128)}) async-done(((f32[1,5120,1280]{2,1,0:T(8,128)}, f32[1,5120,1280]{2,1,0:T(8,128)}, f32[1,5120,1280]{2,1,0:T(8,128)}, f32[1,5120,1280]{2,1,0:T(8,128)}), (f32[1,5120,1280]{2,1,0:T(8,128)}, f32[1,5120,1280]{2,1,0:T(8,128)}, ...) | async-done | bytes 104857616 | tf_op jit(solution)/shard_map/psum | solution.py:51
  3246.7 69.0 %pad_maximum_fusion.1 = f32[4,5120,1280]{2,1,0:T(8,128)} fusion(f32[1,5120,1280]{2,1,0:T(8,128)} %get-tuple-element.8, f32[1,5120,1280]{2,1,0:T(8,128)} %get-tuple-element.9, f32[1,5120,1280]{2,1,0:T(8,128)} %get-tuple-element.10, f32[1,5120,1280]{2,1,0:T(8,128)} %get-tuple-element.11), kind=kLoop, calls=%fused_computation.1 | loop fusion | flops 78643200 | bytes 209715200 | tf_op jit(solution)/shard_map/stack | solution.py:52
  (71 shorter events, 363.2 us)
Async XLA Ops:
  7.2 2081.0 %all-reduce.5.cloned.1.call-start = ((), (), s32[]{:S(2)}) async-start(), calls=%async_computation | async-start | bytes 209715200 | tf_op jit(solution)/shard_map/psum | solution.py:50
  7.2 20.0 copy-start
  74.6 21.6 copy-start.17
  120.9 22.2 copy-start.16
  167.9 1.5 copy-start.15
  216.9 29.5 copy-start.11
  266.6 29.7 copy-start.12
  316.5 29.7 copy-start.14
  346.2 21.2 copy-start.18
  389.3 45.2 %slice-start = ((s8[5242880]{0:T(1024)(128)(4,1)}), s8[4194304]{0:T(1024)(128)(4,1)S(1)}, s32[]{:S(2)}) async-start(s8[5242880]{0:T(1024)(128)(4,1)} %bitcast.194), calls=%async_computation.2 | async-start | bytes 8388608
  411.9 22.6 slice-start.1
  460.4 21.6 copy-start.4
  507.1 22.2 copy-start.3
  554.0 21.5 copy-start.1
  602.0 31.2 copy-start.6
  653.3 29.8 copy-start.9
  703.3 29.8 copy-start.10
  733.1 21.2 copy-start.5
  784.1 29.7 copy-start.2
  843.3 43.0 %copy-start.8 = (bf16[1024,1280]{1,0:T(8,128)(2,1)S(1)}, bf16[1024,1280]{1,0:T(8,128)(2,1)}, u32[]{:S(2)}) copy-start(bf16[1024,1280]{1,0:T(8,128)(2,1)} %add_convert_fusion) | copy-start | bytes 7864324
  931.3 26.6 copy-start.13
  931.3 2315.4 %all-reduce.7.cloned.1.call-start = ((), (), s32[]{:S(2)}) async-start(), calls=%async_computation.1 | async-start | bytes 209715200 | tf_op jit(solution)/shard_map/psum | solution.py:51
  957.9 51.6 %slice-start.2 = ((s8[10485760]{0:T(1024)(128)(4,1)}), s8[4194304]{0:T(1024)(128)(4,1)S(1)}, s32[]{:S(2)}) async-start(s8[10485760]{0:T(1024)(128)(4,1)} %bitcast.196), calls=%async_computation.4 | async-start | bytes 8388608
  957.9 51.6 %slice-start.3 = ((s8[10485760]{0:T(1024)(128)(4,1)}), s8[4194304]{0:T(1024)(128)(4,1)S(1)}, s32[]{:S(2)}) async-start(s8[10485760]{0:T(1024)(128)(4,1)} %bitcast.196), calls=%async_computation.5 | async-start | bytes 8388608
  983.3 26.2 slice-start.4
  1061.1 29.8 copy-start.7
Sparse Core Ops, SparseCore 0:
  931.4 1156.6 all-reduce.4
  2092.3 1154.3 all-reduce.6
where the time goes:
time: 3330 us; the launch traced here: 3320 us
  waiting for transfers between devices  1930 us (58%)
  matrix products  1140 us (34%)
  other arithmetic  138 us (4%)
  local copies, waits for them, and re-layouts  98.6 us (3%)
    psum x1, waiting for transfers between devices, local_step(): grads_out[layer] = lax.psum(grads_out[layer] + g_out, 'data')  993 us
    psum x1, waiting for transfers between devices, local_step(): grads_in[layer] = lax.psum(grads_in[layer] + g_in, 'data')  939 us
    dot_general x8, matrix products, local_step(): lax.dot_general(layer_in, d_pre, CONTRACT_ROWS, preferred_element_type=jn...  244 us
    dot_general x8, matrix products, local_step(): lax.dot_general(gelu_out, cotangent, CONTRACT_ROWS, preferred_element_typ...  217 us
    dot_general x8, matrix products, local_step(): branch = jnp.dot(gelu_out, w_out[layer], preferred_element_type=jnp.float32)  204 us
    dot_general x6, matrix products, local_step(): lax.dot_general(cotangent, w_out[layer], CONTRACT_LAST, preferred_element...  180 us
    dot_general x8, matrix products, local_step(): jnp.dot(hidden, w_in[layer], preferred_element_type=jnp.float32)  172 us
    another operation x2, other arithmetic, local_step(): return (jnp.stack(grads_in), jnp.stack(grads_out))  138 us
  transfers between devices with their start and end apart: 2, of which 2 were waited for; matrix products, arithmetic and copies ran while one was open for 12% of the time, Pallas kernels for 0%

commit v1 on v0

v1 whole, which is shorter than its diff:
```python
import math
import jax
import jax.numpy as jnp
from jax import lax
from jax.experimental import pallas as pl
from jax.sharding import PartitionSpec as P


NN = (((1,), (0,)), ((), ()))
NT = (((1,), (1,)), ((), ()))
TN = (((0,), (0,)), ((), ()))
F32 = jnp.float32
BF16 = jnp.bfloat16
ROOT = math.sqrt(2.0 / math.pi)
CUBIC = 0.044715

LAYERS = 4
SENDS = "XYDEG"
PLACES = {"F": ("F", 0), "Q": ("X", 2), "R": ("E", 1), "T": ("G", 3)}
PIECES = {f"{kind}{layer}": 2 for layer in range(LAYERS) for kind in "AB"} | {"B0": 4}
COST = {"u": 39.7, "d": 33.7, "v": 40.7, "g": 33.7, "grad": 11.8, "sum": 8.5, "place": 5.0, "split": 4.0,
        "act": 112.0, "link": 140.0, "core": 13.0, "wake": 2.0, "ahead": 100.0}


def issue_order(pieces, cost):
    plan = [("X", "h0")]
    for layer in range(LAYERS):
        plan += [("o", "u", layer), ("o", "d", layer)]
        if layer + 1 in (1, 3):
            plan.append(("X", f"h{layer + 1}"))
    plan.append(("X", f"g{LAYERS}"))
    plan += [("f", "u", 0), ("f", "u", 1), ("f", "d", 1), ("f", "u", 2), ("f", "u", 3)]
    for layer in reversed(range(LAYERS)):
        for kind in "AB":
            name = f"{kind}{layer}"
            if kind == "B":
                plan += [("o", "v", layer), ("f", "v", layer)]
            plan += [(name, "s", "o"), (name, "s", "f"), ("D", name), (name, "m", "o"), (name, "m", "f")]
            if pieces[name] > 1:
                plan.append(("S", name))
            plan += [("Y", name, piece) for piece in range(pieces[name])]
        if layer:
            plan += [("o", "g", layer), ("f", "g", layer)]
    needs = {("f", "u", 0): ("X", "h0"), ("f", "u", 1): ("X", "h1"), ("f", "u", 3): ("X", "h3"), (f"A{LAYERS - 1}", "s", "f"): ("X", f"g{LAYERS}")}
    for name in pieces:
        needs[name, "m", "f"] = ("D", name)
    order, landed, free = [], {}, {"X": 0.0, "Y": 0.0}
    clock = 0.0
    summing, passing, placing = [], [], []

    def run(item):
        nonlocal clock
        clock = max(clock, landed.get(needs.get(item), 0.0))
        mark = item[0]
        if mark in PLACES:
            clock += cost["sum" if mark == "F" else "place"] / pieces[item[1]]
        elif mark == "S":
            clock += cost["split"]
        elif mark in pieces:
            clock += cost["grad"]
        else:
            clock += cost[item[1]]
        order.append(item)

    def start(item):
        mark = item[0]
        share = 1 if len(item) == 2 else pieces[item[1]]
        if mark in free:
            length = cost["act"] if item[1] not in pieces else cost["link"] / share
            free[mark] = max(clock, free[mark]) + length
            landed[item] = free[mark] + cost["wake"]
        else:
            landed[item] = clock + cost["core"] / share + cost["wake"]
        order.append(item)
        if mark == "Y":
            summing.append(item[1:])

    def serve():
        busy = False
        for tag in [t for t in summing if landed[("Y", *t)] <= clock]:
            summing.remove(tag)
            run(("F", *tag))
            start(("X", *tag))
            start(("E", *tag))
            passing.append(tag)
            placing.append((("R", *tag), ("E", *tag)))
            busy = True
        for tag in [t for t in passing if landed[("X", *t)] <= clock]:
            passing.remove(tag)
            start(("G", *tag))
            placing.extend([(("Q", *tag), ("X", *tag)), (("T", *tag), ("G", *tag))])
            busy = True
        return busy

    def put():
        for entry in placing:
            if landed[entry[1]] <= clock:
                placing.remove(entry)
                run(entry[0])
                return True
        return False

    for item in plan:
        if item[0] in SENDS:
            start(item)
            continue
        serve()
        while free["Y"] - clock > cost["ahead"] and put():
            serve()
        run(item)
    while summing or passing or placing:
        if not (serve() or put()):
            times = [landed[("Y", *t)] for t in summing] + [landed[("X", *t)] for t in passing] + [landed[e[1]] for e in placing]
            clock = max(clock, min(times))
    return order


def gelu_fn(value):
    return jax.nn.gelu(value, approximate=True)


def gelu_slope(value):
    square = value * value
    t = jnp.tanh(ROOT * value * (1.0 + CUBIC * square))
    plus = 0.5 + 0.5 * t
    return plus + value * plus * (1.0 - t) * (ROOT + 3.0 * ROOT * CUBIC * square)


def dot(left, right, dims):
    return lax.dot_general(left, right, dims, preferred_element_type=F32)


def blank(shape):
    return pl.pallas_call(
        lambda out: None,
        out_shape=jax.ShapeDtypeStruct(shape, F32),
        out_specs=pl.BlockSpec(memory_space=pl.ANY),
    )()


def solution(mesh):
    order = issue_order(PIECES, COST)
    group = mesh.shape["data"]
    to_core = [(i, i ^ 1) for i in range(group)]
    to_x = [(i, i ^ 2) for i in range(group)]
    to_y = [(i, i ^ 4) for i in range(group)]
    route = {"X": to_x, "Y": to_y, "D": to_core, "E": to_core, "G": to_core}

    def local_step(tokens, targets, w_in, w_out):
        rows = tokens.shape[0]
        layers, width, ff = w_in.shape
        blk = ff // 4
        scale = 1.0 / math.sqrt(rows * group)
        me = lax.axis_index("data") & 3
        starts = [pl.multiple_of((me ^ flip) * blk, blk) for flip in range(4)]
        grads = {"A": blank((layers, ff, width)), "B": blank((layers, width, ff))}
        val = {("o", "h0"): tokens}

        def up(side, layer):
            pre = dot(val[side, f"h{layer}"], w_in[layer], NN).astype(BF16)
            act = gelu_fn(pre.astype(F32)).astype(BF16)
            val[side, f"u{layer}"], val[side, f"a{layer}"] = lax.optimization_barrier((pre, act))

        def down(side, layer):
            hidden = val[side, f"h{layer}"].astype(F32) + dot(val[side, f"a{layer}"], w_out[layer], NN)
            hidden = hidden.astype(BF16)
            if layer < layers - 1:
                val[side, f"h{layer + 1}"] = hidden
            else:
                val[side, f"g{layers}"] = ((hidden.astype(F32) - targets.astype(F32)) * scale).astype(BF16)

        def back_act(side, layer):
            cot, pre = lax.optimization_barrier((val[side, f"g{layer + 1}"], val[side, f"u{layer}"]))
            d_act = dot(cot, w_out[layer], NT)
            d_pre = (d_act * gelu_slope(pre.astype(F32))).astype(BF16)
            val[side, f"v{layer}"] = lax.optimization_barrier(d_pre)

        def back_hidden(side, layer):
            total = val[side, f"g{layer + 1}"].astype(F32) + dot(val[side, f"v{layer}"], w_in[layer], NT)
            val[side, f"g{layer}"] = total.astype(BF16)

        def partial_sum(name, block, side):
            kind, layer = name[0], int(name[1])
            start = starts[1] if block == "s" else starts[0]
            if kind == "A":
                left, right = val[side, f"a{layer}"], val[side, f"g{layer + 1}"]
                left = lax.dynamic_slice_in_dim(left, start, blk, axis=1)
            else:
                left, right = val[side, f"h{layer}"], val[side, f"v{layer}"]
                right = lax.dynamic_slice_in_dim(right, start, blk, axis=1)
            total = dot(left, right, TN)
            if side == "f":
                total = total + val[name, block]
                if block == "m":
                    total = total + val["D", name]
            else:
                total = lax.optimization_barrier(total)
            val[name, block] = val[name, 0] = total

        def split(name):
            own = val[name, "m"]
            step = own.shape[0] // PIECES[name]
            for piece in range(PIECES[name]):
                val[name, piece] = own[piece * step:(piece + 1) * step]

        def place(mark, name, piece):
            if mark == "F":
                val["F", name, piece] = val[name, piece] + val["Y", name, piece]
            source, which = PLACES[mark]
            block, start = val[source, name, piece], starts[which]
            kind, layer = name[0], int(name[1])
            first = piece * block.shape[0]
            where = (layer, start + first, 0) if kind == "A" else (layer, first, start)
            grads[kind] = lax.dynamic_update_slice(grads[kind], block[None], where)

        def operation(item):
            mark = item[0]
            if mark in PIECES:
                partial_sum(*item)
            elif mark == "S":
                split(item[1])
            elif mark in PLACES:
                place(*item)
            else:
                {"u": up, "d": down, "v": back_act, "g": back_hidden}[item[1]](mark, item[2])

        def transfer(item):
            mark, rest = item[0], item[1:]
            if rest[0] not in PIECES:
                val["f", rest[0]] = lax.ppermute(val["o", rest[0]], "data", to_x)
                return
            source = {"X": ("F", *rest), "E": ("F", *rest), "G": ("X", *rest), "Y": rest, "D": (rest[0], "s")}[mark]
            val[item] = lax.ppermute(val[source], "data", route[mark])

        for item in order:
            (transfer if item[0] in SENDS else operation)(item)
        return grads["B"], grads["A"]

    return jax.shard_map(local_step, mesh=mesh, in_specs=(P("data"), P("data"), P(), P()), out_specs=(P(), P()), check_vma=False)
```

time: 3330 us -> 3210 us (0.964)
  waiting for transfers between devices: 1930 us -> 1280 us
  matrix products: 1140 us -> 1570 us
  starting transfers between devices: 0.08 us -> 90.2 us
  local copies, waits for them, and re-layouts: 98.6 us -> 183 us
  other arithmetic: 138 us -> 82.5 us
    psum x2 -> x0, waiting for transfers between devices: 1930 us -> none  [the longest x1 993 us: local_step(): grads_out[layer] = lax.psum(grads_out[layer] + g_out, 'data')]
    ppermute x0 -> x84, waiting for transfers between devices: none -> 1280 us  [the longest x80 1280 us: transfer(): val[item] = lax.ppermute(val[source], 'data', route[mark])]
    dot_general x44 -> x59, matrix products: 1140 us -> 1570 us  [dot(): return lax.dot_general(left, right, dims, preferred_element_type=F32)]
    dynamic_update_slice x0 -> x54, local copies, waits for them, and re-layouts: none -> 154 us  [place(): grads[kind] = lax.dynamic_update_slice(grads[kind], block[None], where)]
    another operation x2 -> x0, other arithmetic: 138 us -> none  [local_step(): return (jnp.stack(grads_in), jnp.stack(grads_out))]
    unnamed x49 -> x116, local copies, waits for them, and re-layouts: 98.6 us -> 1.7 us
    ppermute x0 -> x84, starting transfers between devices: none -> 90.2 us  [the longest x80 86.6 us: transfer(): val[item] = lax.ppermute(val[source], 'data', route[mark])]
    dynamic_update_slice x0 -> x18, other arithmetic: none -> 82.5 us  [place(): grads[kind] = lax.dynamic_update_slice(grads[kind], block[None], where)]
  transfers between devices with their start and end apart: 2 -> 84, of which waited for: 2 -> 27; matrix products, arithmetic and copies ran while one was open for 12% -> 48% of each run, Pallas kernels for 0% -> 0%
where the time goes in v1:
time: 3210 us
  matrix products  1570 us (49%)
  waiting for transfers between devices  1280 us (40%)
  local copies, waits for them, and re-layouts  183 us (6%)
  starting transfers between devices  90.2 us (3%)
  other arithmetic  82.5 us (3%)
    dot_general x59, matrix products, dot(): return lax.dot_general(left, right, dims, preferred_element_type=F32)  1570 us
    ppermute x80, waiting for transfers between devices, transfer(): val[item] = lax.ppermute(val[source], 'data', route[mark])  1280 us
    dynamic_update_slice x54, local copies, waits for them, and re-layouts, place(): grads[kind] = lax.dynamic_update_slice(grads[kind], block[None], where)  154 us
    ppermute x80, starting transfers between devices, transfer(): val[item] = lax.ppermute(val[source], 'data', route[mark])  86.6 us
    dynamic_update_slice x18, other arithmetic, place(): grads[kind] = lax.dynamic_update_slice(grads[kind], block[None], where)  82.5 us
  transfers between devices with their start and end apart: 84, of which 27 were waited for; matrix products, arithmetic and copies ran while one was open for 48% of the time, Pallas kernels for 0%

profile of v1, /device:TPU:1, one launch (start us, length us, event | category | flops | bytes accessed | tf_op | source)
XLA Modules:
  0.0 3205.6 jit_solution(5669920305563670807)
XLA Ops:
  2.7 44.6 %fusion.93 = (bf16[2048,5120]{1,0:T(8,128)(2,1)}, bf16[2048,5120]{1,0:T(8,128)(2,1)}) fusion(bf16[2048,1280]{1,0:T(8,128)(2,1)} %param.4, bf16[4,1280,5120]{2,1,0:T(8,128)(2,1)} %param.6), kind=kOutput, calls=%fused_computation.149 | convolution fusion | flops 26958888960 | bytes 60293120 | tf_op jit(solution)/shard_map/dot_general | solution.py:130
  82.6 44.9 %fusion.99 = (bf16[2048,5120]{1,0:T(8,128)(2,1)}, bf16[2048,5120]{1,0:T(8,128)(2,1)}) fusion(bf16[2048,1280]{1,0:T(8,128)(2,1)} %add_convert_fusion.10, bf16[4,1280,5120]{2,1,0:T(8,128)(2,1)} %param.6), kind=kOutput, calls=%fused_computation.155 | convolution fusion | flops 26958888960 | bytes 60293120 | tf_op jit(solution)/shard_map/dot_general | solution.py:130
  163.0 44.4 %fusion.105 = (bf16[2048,5120]{1,0:T(8,128)(2,1)}, bf16[2048,5120]{1,0:T(8,128)(2,1)}) fusion(bf16[2048,1280]{1,0:T(8,128)(2,1)} %add_convert_fusion.9, bf16[4,1280,5120]{2,1,0:T(8,128)(2,1)} %param.6), kind=kOutput, calls=%fused_computation.161 | convolution fusion | flops 26958888960 | bytes 60293120 | tf_op jit(solution)/shard_map/dot_general | solution.py:130
  244.6 44.0 %fusion.111 = (bf16[2048,5120]{1,0:T(8,128)(2,1)}, bf16[2048,5120]{1,0:T(8,128)(2,1)}) fusion(bf16[2048,1280]{1,0:T(8,128)(2,1)} %add_convert_fusion.8, bf16[4,1280,5120]{2,1,0:T(8,128)(2,1)} %param.6), kind=kOutput, calls=%fused_computation.167 | convolution fusion | flops 26958888960 | bytes 60293120 | tf_op jit(solution)/shard_map/dot_general | solution.py:130
  324.9 53.3 %fusion.71 = bf16[2048,5120]{1,0:T(8,128)(2,1)} fusion(bf16[2048,5120]{1,0:T(8,128)(2,1)} %get-tuple-element.43, bf16[2048,1280]{1,0:T(8,128)(2,1)} %multiply_convert_fusion, bf16[4,5120,1280]{2,1,0:T(8,128)(2,1)} %param.7), kind=kOutput, calls=%fused_computation.127 | convolution fusion | flops 27021803520 | bytes 60293120 | tf_op jit(solution)/shard_map/dot_general | solution.py:130
  413.9 52.7 %fusion.55 = bf16[2048,5120]{1,0:T(8,128)(2,1)} fusion(bf16[2048,5120]{1,0:T(8,128)(2,1)} %get-tuple-element.50, bf16[2048,1280]{1,0:T(8,128)(2,1)} %add_convert_fusion.4, bf16[4,5120,1280]{2,1,0:T(8,128)(2,1)} %param.7), kind=kOutput, calls=%fused_computation.111 | convolution fusion | flops 27021803520 | bytes 60293120 | tf_op jit(solution)/shard_map/dot_general | solution.py:130
  502.8 52.8 %fusion.39 = bf16[2048,5120]{1,0:T(8,128)(2,1)} fusion(bf16[2048,5120]{1,0:T(8,128)(2,1)} %get-tuple-element.56, bf16[2048,1280]{1,0:T(8,128)(2,1)} %add_convert_fusion.2, bf16[4,5120,1280]{2,1,0:T(8,128)(2,1)} %param.7), kind=kOutput, calls=%fused_computation.95 | convolution fusion | flops 27021803520 | bytes 60293120 | tf_op jit(solution)/shard_map/dot_general | solution.py:130
  591.3 52.9 %fusion.23 = bf16[2048,5120]{1,0:T(8,128)(2,1)} fusion(bf16[2048,5120]{1,0:T(8,128)(2,1)} %get-tuple-element.62, bf16[2048,1280]{1,0:T(8,128)(2,1)} %add_convert_fusion, bf16[4,5120,1280]{2,1,0:T(8,128)(2,1)} %param.7), kind=kOutput, calls=%fused_computation.79 | convolution fusion | flops 27021803520 | bytes 60293120 | tf_op jit(solution)/shard_map/dot_general | solution.py:130
  826.6 43.8 %fusion.123 = (bf16[2048,5120]{1,0:T(8,128)(2,1)}, bf16[2048,5120]{1,0:T(8,128)(2,1)}) fusion(bf16[2048,1280]{1,0:T(8,128)(2,1)} %collective-permute-done.11, bf16[4,1280,5120]{2,1,0:T(8,128)(2,1)} %param.6), kind=kOutput, calls=%fused_computation.179 | convolution fusion | flops 26958888960 | bytes 60293120 | tf_op jit(solution)/shard_map/dot_general | solution.py:130
  905.2 42.7 %fusion.129 = (bf16[2048,5120]{1,0:T(8,128)(2,1)}, bf16[2048,5120]{1,0:T(8,128)(2,1)}) fusion(bf16[2048,1280]{1,0:T(8,128)(2,1)S(1)} %add_convert_fusion.6, bf16[4,1280,5120]{2,1,0:T(8,128)(2,1)} %param.6), kind=kOutput, calls=%fused_computation.185 | convolution fusion | flops 26958888960 | bytes 60293120 | tf_op jit(solution)/shard_map/dot_general | solution.py:130
  947.9 44.0 %fusion.135 = (bf16[2048,5120]{1,0:T(8,128)(2,1)}, bf16[2048,5120]{1,0:T(8,128)(2,1)}) fusion(bf16[2048,1280]{1,0:T(8,128)(2,1)} %collective-permute-done.30, bf16[4,1280,5120]{2,1,0:T(8,128)(2,1)} %param.6), kind=kOutput, calls=%fused_computation.191 | convolution fusion | flops 26958888960 | bytes 60293120 | tf_op jit(solution)/shard_map/dot_general | solution.py:130
  991.9 44.2 %fusion.117 = (bf16[2048,5120]{1,0:T(8,128)(2,1)}, bf16[2048,5120]{1,0:T(8,128)(2,1)}) fusion(bf16[2048,1280]{1,0:T(8,128)(2,1)} %collective-permute-done, bf16[4,1280,5120]{2,1,0:T(8,128)(2,1)} %param.6), kind=kOutput, calls=%fused_computation.173 | convolution fusion | flops 26958888960 | bytes 60293120 | tf_op jit(solution)/shard_map/dot_general | solution.py:130
  1036.1 53.3 %fusion.79 = bf16[2048,5120]{1,0:T(8,128)(2,1)} fusion(bf16[2048,5120]{1,0:T(8,128)(2,1)} %get-tuple-element.40, bf16[2048,1280]{1,0:T(8,128)(2,1)} %collective-permute-done.1, bf16[4,5120,1280]{2,1,0:T(8,128)(2,1)} %param.7), kind=kOutput, calls=%fused_computation.135 | convolution fusion | flops 27021803520 | bytes 60293120 | tf_op jit(solution)/shard_map/dot_general | solution.py:130
  1125.2 52.8 %fusion.63 = bf16[2048,5120]{1,0:T(8,128)(2,1)} fusion(bf16[2048,5120]{1,0:T(8,128)(2,1)} %get-tuple-element.47, bf16[2048,1280]{1,0:T(8,128)(2,1)} %add_convert_fusion.5, bf16[4,5120,1280]{2,1,0:T(8,128)(2,1)} %param.7), kind=kOutput, calls=%fused_computation.119 | convolution fusion | flops 27021803520 | bytes 60293120 | tf_op jit(solution)/shard_map/dot_general | solution.py:130
  1214.1 52.7 %fusion.47 = bf16[2048,5120]{1,0:T(8,128)(2,1)} fusion(bf16[2048,5120]{1,0:T(8,128)(2,1)} %get-tuple-element.53, bf16[2048,1280]{1,0:T(8,128)(2,1)} %add_convert_fusion.3, bf16[4,5120,1280]{2,1,0:T(8,128)(2,1)} %param.7), kind=kOutput, calls=%fused_computation.103 | convolution fusion | flops 27021803520 | bytes 60293120 | tf_op jit(solution)/shard_map/dot_general | solution.py:130
  1366.4 53.2 %fusion.31 = bf16[2048,5120]{1,0:T(8,128)(2,1)} fusion(bf16[2048,5120]{1,0:T(8,128)(2,1)} %get-tuple-element.59, bf16[2048,1280]{1,0:T(8,128)(2,1)} %add_convert_fusion.1, bf16[4,5120,1280]{2,1,0:T(8,128)(2,1)} %param.7), kind=kOutput, calls=%fused_computation.87 | convolution fusion | flops 27021803520 | bytes 60293120 | tf_op jit(solution)/shard_map/dot_general | solution.py:130
  1600.7 45.3 %collective-permute-done.3 = f32[640,1280]{1,0:T(8,128)} collective-permute-done((f32[640,1280]{1,0:T(8,128)}, f32[640,1280]{1,0:T(8,128)}, u32[]{:S(2)}, u32[]{:S(2)}) %collective-permute-start.3) | collective-permute-done | bytes 3276832 | tf_op jit(solution)/shard_map/ppermute | solution.py:233
  1729.2 57.2 %collective-permute-done.5 = f32[640,1280]{1,0:T(8,128)} collective-permute-done((f32[640,1280]{1,0:T(8,128)S(1)}, f32[640,1280]{1,0:T(8,128)}, u32[]{:S(2)}, u32[]{:S(2)}) %collective-permute-start.5) | collective-permute-done | bytes 3276832 | tf_op jit(solution)/shard_map/ppermute | solution.py:233
  1829.4 54.7 %collective-permute-done.55 = f32[640,1280]{1,0:T(8,128)} collective-permute-done((f32[640,1280]{1,0:T(8,128)}, f32[640,1280]{1,0:T(8,128)}, u32[]{:S(2)}, u32[]{:S(2)}) %collective-permute-start.55) | collective-permute-done | bytes 3276832 | tf_op jit(solution)/shard_map/ppermute | solution.py:233
  1902.4 51.9 %collective-permute-done.9 = f32[640,1280]{1,0:T(8,128)} collective-permute-done((f32[640,1280]{1,0:T(8,128)}, f32[640,1280]{1,0:T(8,128)}, u32[]{:S(2)}, u32[]{:S(2)}) %collective-permute-start.9) | collective-permute-done | bytes 3276832 | tf_op jit(solution)/shard_map/ppermute | solution.py:233
  1966.0 59.9 %collective-permute-done.59 = f32[640,1280]{1,0:T(8,128)} collective-permute-done((f32[640,1280]{1,0:T(8,128)S(1)}, f32[640,1280]{1,0:T(8,128)}, u32[]{:S(2)}, u32[]{:S(2)}) %collective-permute-start.59) | collective-permute-done | bytes 3276832 | tf_op jit(solution)/shard_map/ppermute | solution.py:233
  2042.6 123.8 %collective-permute-done.13 = f32[640,1280]{1,0:T(8,128)} collective-permute-done((f32[640,1280]{1,0:T(8,128)}, f32[640,1280]{1,0:T(8,128)}, u32[]{:S(2)}, u32[]{:S(2)}) %collective-permute-start.13) | collective-permute-done | bytes 3276832 | tf_op jit(solution)/shard_map/ppermute | solution.py:233
  2194.4 47.9 %collective-permute-done.17 = f32[640,1280]{1,0:T(8,128)} collective-permute-done((f32[640,1280]{1,0:T(8,128)}, f32[640,1280]{1,0:T(8,128)}, u32[]{:S(2)}, u32[]{:S(2)}) %collective-permute-start.17) | collective-permute-done | bytes 3276832 | tf_op jit(solution)/shard_map/ppermute | solution.py:233
  2251.5 61.0 %collective-permute-done.62 = f32[640,1280]{1,0:T(8,128)} collective-permute-done((f32[640,1280]{1,0:T(8,128)}, f32[640,1280]{1,0:T(8,128)}, u32[]{:S(2)}, u32[]{:S(2)}) %collective-permute-start.62) | collective-permute-done | bytes 3276832 | tf_op jit(solution)/shard_map/ppermute | solution.py:233
  2316.4 66.3 %collective-permute-done.19 = f32[640,1280]{1,0:T(8,128)} collective-permute-done((f32[640,1280]{1,0:T(8,128)}, f32[640,1280]{1,0:T(8,128)}, u32[]{:S(2)}, u32[]{:S(2)}) %collective-permute-start.19) | collective-permute-done | bytes 3276832 | tf_op jit(solution)/shard_map/ppermute | solution.py:233
  2404.1 48.5 %collective-permute-done.64 = f32[640,1280]{1,0:T(8,128)} collective-permute-done((f32[640,1280]{1,0:T(8,128)}, f32[640,1280]{1,0:T(8,128)}, u32[]{:S(2)}, u32[]{:S(2)}) %collective-permute-start.64) | collective-permute-done | bytes 3276832 | tf_op jit(solution)/shard_map/ppermute | solution.py:233
  2480.1 60.6 %collective-permute-done.67 = f32[640,1280]{1,0:T(8,128)} collective-permute-done((f32[640,1280]{1,0:T(8,128)}, f32[640,1280]{1,0:T(8,128)}, u32[]{:S(2)}, u32[]{:S(2)}) %collective-permute-start.67) | collective-permute-done | bytes 3276832 | tf_op jit(solution)/shard_map/ppermute | solution.py:233
  2552.7 58.2 %collective-permute-done.68 = f32[640,1280]{1,0:T(8,128)} collective-permute-done((f32[640,1280]{1,0:T(8,128)}, f32[640,1280]{1,0:T(8,128)}, u32[]{:S(2)}, u32[]{:S(2)}) %collective-permute-start.68) | collective-permute-done | bytes 3276832 | tf_op jit(solution)/shard_map/ppermute | solution.py:233
  2637.0 50.0 %collective-permute-done.71 = f32[640,1280]{1,0:T(8,128)} collective-permute-done((f32[640,1280]{1,0:T(8,128)}, f32[640,1280]{1,0:T(8,128)}, u32[]{:S(2)}, u32[]{:S(2)}) %collective-permute-start.71) | collective-permute-done | bytes 3276832 | tf_op jit(solution)/shard_map/ppermute | solution.py:233
  2772.4 56.2 %collective-permute-done.34 = f32[320,1280]{1,0:T(8,128)} collective-permute-done((f32[320,1280]{1,0:T(8,128)S(1)}, f32[320,1280]{1,0:T(8,128)}, u32[]{:S(2)}, u32[]{:S(2)}) %collective-permute-start.34) | collective-permute-done | bytes 1638432 | tf_op jit(solution)/shard_map/ppermute | solution.py:233
  2839.9 58.9 %collective-permute-done.76 = f32[640,1280]{1,0:T(8,128)} collective-permute-done((f32[640,1280]{1,0:T(8,128)S(1)}, f32[640,1280]{1,0:T(8,128)}, u32[]{:S(2)}, u32[]{:S(2)}) %collective-permute-start.76) | collective-permute-done | bytes 3276832 | tf_op jit(solution)/shard_map/ppermute | solution.py:233
  3020.4 63.4 %collective-permute-done.80 = f32[640,1280]{1,0:T(8,128)S(1)} collective-permute-done((f32[640,1280]{1,0:T(8,128)S(1)}, f32[640,1280]{1,0:T(8,128)S(1)}, u32[]{:S(2)}, u32[]{:S(2)}) %collective-permute-start.80) | collective-permute-done | bytes 3276832 | tf_op jit(solution)/shard_map/ppermute | solution.py:233
  (414 shorter events, 1464.0 us)
Async XLA Ops:
  0.6 947.2 %collective-permute-start.30 = (bf16[2048,1280]{1,0:T(8,128)(2,1)}, bf16[2048,1280]{1,0:T(8,128)(2,1)}, u32[]{:S(2)}, u32[]{:S(2)}) collective-permute-start(bf16[2048,1280]{1,0:T(8,128)(2,1)} %param.4), channel_id=1, source_target_pairs={{0,2},{1,3},{2,0},{3,1},{4,6},{5,7},{6,4},{7,5}} | collective-permute-start | bytes 15728648 | tf_op jit(solution)/shard_map/ppermute | solution.py:230
  82.6 744.0 %collective-permute-start.11 = (bf16[2048,1280]{1,0:T(8,128)(2,1)}, bf16[2048,1280]{1,0:T(8,128)(2,1)}, u32[]{:S(2)}, u32[]{:S(2)}) collective-permute-start(bf16[2048,1280]{1,0:T(8,128)(2,1)} %add_convert_fusion.10), channel_id=1, source_target_pairs={{0,2},{1,3},{2,0},{3,1},{4,6},{5,7},{6,4},{7,5}} | collective-permute-start | bytes 15728648 | tf_op jit(solution)/shard_map/ppermute | solution.py:230
  243.2 748.8 %collective-permute-start = (bf16[2048,1280]{1,0:T(8,128)(2,1)}, bf16[2048,1280]{1,0:T(8,128)(2,1)}, u32[]{:S(2)}, u32[]{:S(2)}) collective-permute-start(bf16[2048,1280]{1,0:T(8,128)(2,1)} %add_convert_fusion.8), channel_id=1, source_target_pairs={{0,2},{1,3},{2,0},{3,1},{4,6},{5,7},{6,4},{7,5}} | collective-permute-start | bytes 15728648 | tf_op jit(solution)/shard_map/ppermute | solution.py:230
  324.8 711.3 %collective-permute-start.1 = (bf16[2048,1280]{1,0:T(8,128)(2,1)}, bf16[2048,1280]{1,0:T(8,128)(2,1)}, u32[]{:S(2)}, u32[]{:S(2)}) collective-permute-start(bf16[2048,1280]{1,0:T(8,128)(2,1)} %multiply_convert_fusion), channel_id=1, source_target_pairs={{0,2},{1,3},{2,0},{3,1},{4,6},{5,7},{6,4},{7,5}} | collective-permute-start | bytes 15728648 | tf_op jit(solution)/shard_map/ppermute | solution.py:230
  1354.6 148.6 %collective-permute-start.2 = (f32[1280,1280]{1,0:T(8,128)}, f32[1280,1280]{1,0:T(8,128)}, u32[]{:S(2)}, u32[]{:S(2)}) collective-permute-start(f32[1280,1280]{1,0:T(8,128)} %convolution_add_fusion.12), channel_id=1, source_target_pairs={{0,1},{1,0},{2,3},{3,2},{4,5},{5,4},{6,7},{7,6}} | collective-permute-start | bytes 19660808 | tf_op jit(solution)/shard_map/ppermute | solution.py:233
  1365.9 217.4 %collective-permute-start.12 = (f32[1280,1280]{1,0:T(8,128)}, f32[1280,1280]{1,0:T(8,128)}, u32[]{:S(2)}, u32[]{:S(2)}) collective-permute-start(f32[1280,1280]{1,0:T(8,128)} %convolution_add_fusion.10), channel_id=1, source_target_pairs={{0,1},{1,0},{2,3},{3,2},{4,5},{5,4},{6,7},{7,6}} | collective-permute-start | bytes 19660808 | tf_op jit(solution)/shard_map/ppermute | solution.py:233
  1458.0 195.5 %collective-permute-start.21 = (f32[1280,1280]{1,0:T(8,128)}, f32[1280,1280]{1,0:T(8,128)}, u32[]{:S(2)}, u32[]{:S(2)}) collective-permute-start(f32[1280,1280]{1,0:T(8,128)} %convolution_add_fusion.8), channel_id=1, source_target_pairs={{0,1},{1,0},{2,3},{3,2},{4,5},{5,4},{6,7},{7,6}} | collective-permute-start | bytes 19660808 | tf_op jit(solution)/shard_map/ppermute | solution.py:233
  1488.0 304.8 %collective-permute-start.31 = (f32[1280,1280]{1,0:T(8,128)}, f32[1280,1280]{1,0:T(8,128)}, u32[]{:S(2)}, u32[]{:S(2)}) collective-permute-start(f32[1280,1280]{1,0:T(8,128)} %fusion.202), channel_id=1, source_target_pairs={{0,1},{1,0},{2,3},{3,2},{4,5},{5,4},{6,7},{7,6}} | collective-permute-start | bytes 19660808 | tf_op jit(solution)/shard_map/ppermute | solution.py:233
  1575.8 140.4 %collective-permute-start.51 = (f32[640,1280]{1,0:T(8,128)}, f32[640,1280]{1,0:T(8,128)}, u32[]{:S(2)}, u32[]{:S(2)}) collective-permute-start(f32[640,1280]{1,0:T(8,128)} %get-tuple-element.108), channel_id=1, source_target_pairs={{0,4},{1,5},{2,6},{3,7},{4,0},{5,1},{6,2},{7,3}} | collective-permute-start | bytes 9830408 | tf_op jit(solution)/shard_map/ppermute | solution.py:233
  1646.0 140.4 %collective-permute-start.5 = (f32[640,1280]{1,0:T(8,128)S(1)}, f32[640,1280]{1,0:T(8,128)}, u32[]{:S(2)}, u32[]{:S(2)}) collective-permute-start(f32[640,1280]{1,0:T(8,128)S(1)} %copy-done.3), channel_id=1, source_target_pairs={{0,4},{1,5},{2,6},{3,7},{4,0},{5,1},{6,2},{7,3}} | collective-permute-start | bytes 9830408 | tf_op jit(solution)/shard_map/ppermute | solution.py:233
  1670.8 143.8 %collective-permute-start.53 = (f32[640,1280]{1,0:T(8,128)}, f32[640,1280]{1,0:T(8,128)}, u32[]{:S(2)}, u32[]{:S(2)}) collective-permute-start(f32[640,1280]{1,0:T(8,128)} %get-tuple-element.81), channel_id=1, source_target_pairs={{0,2},{1,3},{2,0},{3,1},{4,6},{5,7},{6,4},{7,5}} | collective-permute-start | bytes 9830408 | tf_op jit(solution)/shard_map/ppermute | solution.py:233
  1820.6 133.7 %collective-permute-start.9 = (f32[640,1280]{1,0:T(8,128)}, f32[640,1280]{1,0:T(8,128)}, u32[]{:S(2)}, u32[]{:S(2)}) collective-permute-start(f32[640,1280]{1,0:T(8,128)} %get-tuple-element.99), channel_id=1, source_target_pairs={{0,2},{1,3},{2,0},{3,1},{4,6},{5,7},{6,4},{7,5}} | collective-permute-start | bytes 9830408 | tf_op jit(solution)/shard_map/ppermute | solution.py:233
  1954.3 221.9 %collective-permute-start.14 = (f32[640,1280]{1,0:T(8,128)}, f32[640,1280]{1,0:T(8,128)}, u32[]{:S(2)}, u32[]{:S(2)}) collective-permute-start(f32[640,1280]{1,0:T(8,128)} %get-tuple-element.116), channel_id=1, source_target_pairs={{0,4},{1,5},{2,6},{3,7},{4,0},{5,1},{6,2},{7,3}} | collective-permute-start | bytes 9830408 | tf_op jit(solution)/shard_map/ppermute | solution.py:233
  1957.4 209.0 %collective-permute-start.13 = (f32[640,1280]{1,0:T(8,128)}, f32[640,1280]{1,0:T(8,128)}, u32[]{:S(2)}, u32[]{:S(2)}) collective-permute-start(f32[640,1280]{1,0:T(8,128)} %get-tuple-element.117), channel_id=1, source_target_pairs={{0,4},{1,5},{2,6},{3,7},{4,0},{5,1},{6,2},{7,3}} | collective-permute-start | bytes 9830408 | tf_op jit(solution)/shard_map/ppermute | solution.py:233
  2031.2 152.7 %collective-permute-start.61 = (f32[640,1280]{1,0:T(8,128)}, f32[640,1280]{1,0:T(8,128)}, u32[]{:S(2)}, u32[]{:S(2)}) collective-permute-start(f32[640,1280]{1,0:T(8,128)} %get-tuple-element.75), channel_id=1, source_target_pairs={{0,1},{1,0},{2,3},{3,2},{4,5},{5,4},{6,7},{7,6}} | collective-permute-start | bytes 9830408 | tf_op jit(solution)/shard_map/ppermute | solution.py:233
  2038.7 149.4 %collective-permute-start.60 = (f32[640,1280]{1,0:T(8,128)}, f32[640,1280]{1,0:T(8,128)}, u32[]{:S(2)}, u32[]{:S(2)}) collective-permute-start(f32[640,1280]{1,0:T(8,128)} %get-tuple-element.77), channel_id=1, source_target_pairs={{0,1},{1,0},{2,3},{3,2},{4,5},{5,4},{6,7},{7,6}} | collective-permute-start | bytes 9830408 | tf_op jit(solution)/shard_map/ppermute | solution.py:233
  2175.5 137.0 %collective-permute-start.62 = (f32[640,1280]{1,0:T(8,128)}, f32[640,1280]{1,0:T(8,128)}, u32[]{:S(2)}, u32[]{:S(2)}) collective-permute-start(f32[640,1280]{1,0:T(8,128)} %get-tuple-element.77), channel_id=1, source_target_pairs={{0,2},{1,3},{2,0},{3,1},{4,6},{5,7},{6,4},{7,5}} | collective-permute-start | bytes 9830408 | tf_op jit(solution)/shard_map/ppermute | solution.py:233
  2176.2 207.2 %collective-permute-start.15 = (f32[640,1280]{1,0:T(8,128)}, f32[640,1280]{1,0:T(8,128)}, u32[]{:S(2)}, u32[]{:S(2)}) collective-permute-start(f32[640,1280]{1,0:T(8,128)} %get-tuple-element.97), channel_id=1, source_target_pairs={{0,1},{1,0},{2,3},{3,2},{4,5},{5,4},{6,7},{7,6}} | collective-permute-start | bytes 9830408 | tf_op jit(solution)/shard_map/ppermute | solution.py:233
  2183.9 198.8 %collective-permute-start.19 = (f32[640,1280]{1,0:T(8,128)}, f32[640,1280]{1,0:T(8,128)}, u32[]{:S(2)}, u32[]{:S(2)}) collective-permute-start(f32[640,1280]{1,0:T(8,128)} %get-tuple-element.95), channel_id=1, source_target_pairs={{0,2},{1,3},{2,0},{3,1},{4,6},{5,7},{6,4},{7,5}} | collective-permute-start | bytes 9830408 | tf_op jit(solution)/shard_map/ppermute | solution.py:233
  2188.1 202.4 %collective-permute-start.16 = (f32[640,1280]{1,0:T(8,128)}, f32[640,1280]{1,0:T(8,128)}, u32[]{:S(2)}, u32[]{:S(2)}) collective-permute-start(f32[640,1280]{1,0:T(8,128)} %get-tuple-element.95), channel_id=1, source_target_pairs={{0,1},{1,0},{2,3},{3,2},{4,5},{5,4},{6,7},{7,6}} | collective-permute-start | bytes 9830408 | tf_op jit(solution)/shard_map/ppermute | solution.py:233
  2242.3 156.0 %collective-permute-start.18 = (f32[640,1280]{1,0:T(8,128)}, f32[640,1280]{1,0:T(8,128)S(1)}, u32[]{:S(2)}, u32[]{:S(2)}) collective-permute-start(f32[640,1280]{1,0:T(8,128)} %collective-permute-done.17), channel_id=1, source_target_pairs={{0,1},{1,0},{2,3},{3,2},{4,5},{5,4},{6,7},{7,6}} | collective-permute-start | bytes 9830408 | tf_op jit(solution)/shard_map/ppermute | solution.py:233
  2312.5 146.1 %collective-permute-start.22 = (f32[640,1280]{1,0:T(8,128)}, f32[640,1280]{1,0:T(8,128)}, u32[]{:S(2)}, u32[]{:S(2)}) collective-permute-start(f32[640,1280]{1,0:T(8,128)} %get-tuple-element.115), channel_id=1, source_target_pairs={{0,4},{1,5},{2,6},{3,7},{4,0},{5,1},{6,2},{7,3}} | collective-permute-start | bytes 9830408 | tf_op jit(solution)/shard_map/ppermute | solution.py:233
  2458.6 152.3 %collective-permute-start.68 = (f32[640,1280]{1,0:T(8,128)}, f32[640,1280]{1,0:T(8,128)}, u32[]{:S(2)}, u32[]{:S(2)}) collective-permute-start(f32[640,1280]{1,0:T(8,128)} %get-tuple-element.104), channel_id=1, source_target_pairs={{0,4},{1,5},{2,6},{3,7},{4,0},{5,1},{6,2},{7,3}} | collective-permute-start | bytes 9830408 | tf_op jit(solution)/shard_map/ppermute | solution.py:233
  2465.2 149.0 %collective-permute-start.24 = (f32[640,1280]{1,0:T(8,128)}, f32[640,1280]{1,0:T(8,128)}, u32[]{:S(2)}, u32[]{:S(2)}) collective-permute-start(f32[640,1280]{1,0:T(8,128)} %get-tuple-element.93), channel_id=1, source_target_pairs={{0,1},{1,0},{2,3},{3,2},{4,5},{5,4},{6,7},{7,6}} | collective-permute-start | bytes 9830408 | tf_op jit(solution)/shard_map/ppermute | solution.py:233
  2470.5 144.4 %collective-permute-start.26 = (f32[640,1280]{1,0:T(8,128)}, f32[640,1280]{1,0:T(8,128)}, u32[]{:S(2)}, u32[]{:S(2)}) collective-permute-start(f32[640,1280]{1,0:T(8,128)} %get-tuple-element.93), channel_id=1, source_target_pairs={{0,2},{1,3},{2,0},{3,1},{4,6},{5,7},{6,4},{7,5}} | collective-permute-start | bytes 9830408 | tf_op jit(solution)/shard_map/ppermute | solution.py:233
  2696.4 243.1 %collective-permute-start.77 = (f32[640,1280]{1,0:T(8,128)S(1)}, f32[640,1280]{1,0:T(8,128)S(1)}, u32[]{:S(2)}, u32[]{:S(2)}) collective-permute-start(f32[640,1280]{1,0:T(8,128)S(1)} %get-tuple-element.102), channel_id=1, source_target_pairs={{0,4},{1,5},{2,6},{3,7},{4,0},{5,1},{6,2},{7,3}} | collective-permute-start | bytes 9830408 | tf_op jit(solution)/shard_map/ppermute | solution.py:233
  2769.1 133.8 %collective-permute-start.38 = (f32[320,1280]{1,0:T(8,128)}, f32[320,1280]{1,0:T(8,128)}, u32[]{:S(2)}, u32[]{:S(2)}) collective-permute-start(f32[320,1280]{1,0:T(8,128)} %get-tuple-element.89), channel_id=1, source_target_pairs={{0,2},{1,3},{2,0},{3,1},{4,6},{5,7},{6,4},{7,5}} | collective-permute-start | bytes 4915208 | tf_op jit(solution)/shard_map/ppermute | solution.py:233
  2943.2 140.7 %collective-permute-start.80 = (f32[640,1280]{1,0:T(8,128)S(1)}, f32[640,1280]{1,0:T(8,128)S(1)}, u32[]{:S(2)}, u32[]{:S(2)}) collective-permute-start(f32[640,1280]{1,0:T(8,128)S(1)} %get-tuple-element.69), channel_id=1, source_target_pairs={{0,2},{1,3},{2,0},{3,1},{4,6},{5,7},{6,4},{7,5}} | collective-permute-start | bytes 9830408 | tf_op jit(solution)/shard_map/ppermute | solution.py:233
  2980.5 138.5 %collective-permute-start.42 = (f32[320,1280]{1,0:T(8,128)}, f32[320,1280]{1,0:T(8,128)S(1)}, u32[]{:S(2)}, u32[]{:S(2)}) collective-permute-start(f32[320,1280]{1,0:T(8,128)} %get-tuple-element.87), channel_id=1, source_target_pairs={{0,2},{1,3},{2,0},{3,1},{4,6},{5,7},{6,4},{7,5}} | collective-permute-start | bytes 4915208 | tf_op jit(solution)/shard_map/ppermute | solution.py:233
  2982.6 171.4 %collective-permute-start.44 = (f32[320,1280]{1,0:T(8,128)}, f32[320,1280]{1,0:T(8,128)S(1)}, u32[]{:S(2)}, u32[]{:S(2)}) collective-permute-start(f32[320,1280]{1,0:T(8,128)} %get-tuple-element.85), channel_id=1, source_target_pairs={{0,2},{1,3},{2,0},{3,1},{4,6},{5,7},{6,4},{7,5}} | collective-permute-start | bytes 4915208 | tf_op jit(solution)/shard_map/ppermute | solution.py:233
  3013.6 142.8 %collective-permute-start.41 = (f32[320,1280]{1,0:T(8,128)S(1)}, f32[320,1280]{1,0:T(8,128)S(1)}, u32[]{:S(2)}, u32[]{:S(2)}) collective-permute-start(f32[320,1280]{1,0:T(8,128)S(1)} %get-tuple-element.83), channel_id=1, source_target_pairs={{0,1},{1,0},{2,3},{3,2},{4,5},{5,4},{6,7},{7,6}} | collective-permute-start | bytes 4915208 | tf_op jit(solution)/shard_map/ppermute | solution.py:233
  3015.9 173.2 %collective-permute-start.46 = (f32[320,1280]{1,0:T(8,128)S(1)}, f32[320,1280]{1,0:T(8,128)S(1)}, u32[]{:S(2)}, u32[]{:S(2)}) collective-permute-start(f32[320,1280]{1,0:T(8,128)S(1)} %get-tuple-element.83), channel_id=1, source_target_pairs={{0,2},{1,3},{2,0},{3,1},{4,6},{5,7},{6,4},{7,5}} | collective-permute-start | bytes 4915208 | tf_op jit(solution)/shard_map/ppermute | solution.py:233
  (110 other events, 6524.1 us)

commit v2 on v1

--- a/solution.py
+++ b/solution.py
@@ -3,6 +3,7 @@
 import jax.numpy as jnp
 from jax import lax
 from jax.experimental import pallas as pl
+from jax.experimental.pallas import tpu as pltpu
 from jax.sharding import PartitionSpec as P
 
 
@@ -18,32 +19,34 @@
 SENDS = "XYDEG"
 PLACES = {"F": ("F", 0), "Q": ("X", 2), "R": ("E", 1), "T": ("G", 3)}
 PIECES = {f"{kind}{layer}": 2 for layer in range(LAYERS) for kind in "AB"} | {"B0": 4}
-COST = {"u": 39.7, "d": 33.7, "v": 40.7, "g": 33.7, "grad": 11.8, "sum": 8.5, "place": 5.0, "split": 4.0,
-        "act": 112.0, "link": 140.0, "core": 13.0, "wake": 2.0, "ahead": 100.0}
+COST = {"u": 32.0, "d": 32.0, "v": 39.0, "g": 32.0, "grad": 18.0, "sum": 11.0, "place": 7.5,
+        "act": 112.0, "link": 140.0, "core": 13.0, "wake": 2.0, "ahead": 250.0}
+
+
+def sums(name, pieces, after, between):
+    sends = [("Y", name, piece) for piece in range(pieces[name])]
+    return [(name, "s"), ("D", name), *between[:1], (name, "m"), *sends, *between[1:], *after]
 
 
 def issue_order(pieces, cost):
     plan = [("X", "h0")]
     for layer in range(LAYERS):
         plan += [("o", "u", layer), ("o", "d", layer)]
-        if layer + 1 in (1, 3):
-            plan.append(("X", f"h{layer + 1}"))
+        if layer == 1:
+            plan.append(("X", "h2"))
     plan.append(("X", f"g{LAYERS}"))
-    plan += [("f", "u", 0), ("f", "u", 1), ("f", "d", 1), ("f", "u", 2), ("f", "u", 3)]
+    plan += [("f", "u", 2), ("f", "d", 2), ("f", "u", 3)]
     for layer in reversed(range(LAYERS)):
-        for kind in "AB":
-            name = f"{kind}{layer}"
-            if kind == "B":
-                plan += [("o", "v", layer), ("f", "v", layer)]
-            plan += [(name, "s", "o"), (name, "s", "f"), ("D", name), (name, "m", "o"), (name, "m", "f")]
-            if pieces[name] > 1:
-                plan.append(("S", name))
-            plan += [("Y", name, piece) for piece in range(pieces[name])]
-        if layer:
-            plan += [("o", "g", layer), ("f", "g", layer)]
-    needs = {("f", "u", 0): ("X", "h0"), ("f", "u", 1): ("X", "h1"), ("f", "u", 3): ("X", "h3"), (f"A{LAYERS - 1}", "s", "f"): ("X", f"g{LAYERS}")}
+        one, two = f"A{layer}", f"B{layer}"
+        fill = [("o", "v", layer), ("f", "v", layer)]
+        plan += sums(one, pieces, fill if layer == LAYERS - 1 else [], fill if layer < LAYERS - 1 else [])
+        fill = [("o", "g", layer), ("f", "g", layer)] if layer else []
+        if layer == LAYERS - 2:
+            fill += [("f", "u", 0), ("f", "d", 0), ("f", "u", 1)]
+        plan += sums(two, pieces, [], fill)
+    needs = {("f", "u", 2): ("X", "h2"), ("f", "u", 0): ("X", "h0"), (f"A{LAYERS - 1}", "s"): ("X", f"g{LAYERS}")}
     for name in pieces:
-        needs[name, "m", "f"] = ("D", name)
+        needs[name, "m"] = ("D", name)
     order, landed, free = [], {}, {"X": 0.0, "Y": 0.0}
     clock = 0.0
     summing, passing, placing = [], [], []
@@ -54,8 +57,6 @@
         mark = item[0]
         if mark in PLACES:
             clock += cost["sum" if mark == "F" else "place"] / pieces[item[1]]
-        elif mark == "S":
-            clock += cost["split"]
         elif mark in pieces:
             clock += cost["grad"]
         else:
@@ -121,9 +122,8 @@
 
 def gelu_slope(value):
     square = value * value
-    t = jnp.tanh(ROOT * value * (1.0 + CUBIC * square))
-    plus = 0.5 + 0.5 * t
-    return plus + value * plus * (1.0 - t) * (ROOT + 3.0 * ROOT * CUBIC * square)
+    t = jnp.tanh(value * (ROOT + (ROOT * CUBIC) * square))
+    return (0.5 + 0.5 * t) + (value * (0.5 * ROOT + (1.5 * ROOT * CUBIC) * square)) * (1.0 - t * t)
 
 
 def dot(left, right, dims):
@@ -136,6 +136,197 @@
         out_shape=jax.ShapeDtypeStruct(shape, F32),
         out_specs=pl.BlockSpec(memory_space=pl.ANY),
     )()
+
+
+PARAMS = pltpu.CompilerParams(vmem_limit_bytes=67_043_328)
+
+
+def work(rows, depth, columns, moved):
+    return pl.CostEstimate(flops=2 * rows * depth * columns, bytes_accessed=moved, transcendentals=0)
+
+
+def up_kernel(layer, hidden, w_in):
+    rows, width = hidden.shape
+    ff = w_in.shape[2]
+    tile, chunk = 512, 128
+
+    def body(h_ref, w_ref, u_ref, a_ref):
+        last = None
+        for first in [*range(0, rows, chunk), None]:
+            if first is not None:
+                part = pl.ds(first, chunk)
+                u_ref[part, :] = dot(h_ref[part, :], w_ref[0], NN).astype(BF16)
+            if last is not None:
+                part = pl.ds(last, chunk)
+                a_ref[part, :] = gelu_fn(u_ref[part, :].astype(F32)).astype(BF16)
+            last = first
+
+    return pl.pallas_call(
+        body,
+        grid=(ff // tile,),
+        in_specs=[pl.BlockSpec((rows, width), lambda j: (0, 0)), pl.BlockSpec((1, width, tile), lambda j: (layer, 0, j))],
+        out_specs=[pl.BlockSpec((rows, tile), lambda j: (0, j))] * 2,
+        out_shape=[jax.ShapeDtypeStruct((rows, ff), BF16)] * 2,
+        compiler_params=PARAMS,
+        cost_estimate=work(rows, width, ff, 60_000_000),
+    )(hidden, w_in)
+
+
+def down_kernel(layer, value, weights, base, dims, target=None, scale=1.0):
+    rows, ff = value.shape
+    width = base.shape[1]
+    tile = 512
+    chunk = 128 if dims == NN else 256
+    steps = ff // tile
+    if dims == NN:
+        w_spec = pl.BlockSpec((1, tile, width), lambda j: (layer, j, 0))
+    else:
+        w_spec = pl.BlockSpec((1, width, tile), lambda j: (layer, 0, j))
+    whole = pl.BlockSpec((rows, width), lambda j: (0, 0))
+
+    def body(x_ref, w_ref, base_ref, *rest):
+        out_ref, total = rest[-2:]
+        step = pl.program_id(0)
+
+        @pl.when(step == 0)
+        def _():
+            total[...] = base_ref[...].astype(F32)
+
+        for first in range(0, rows, chunk):
+            part = pl.ds(first, chunk)
+            total[part, :] += dot(x_ref[part, :], w_ref[0], dims)
+
+        @pl.when(step == steps - 1)
+        def _():
+            result = total[...].astype(BF16)
+            if target is not None:
+                result = ((result.astype(F32) - rest[0][...].astype(F32)) * scale).astype(BF16)
+            out_ref[...] = result
+
+    extra = [] if target is None else [target]
+    return pl.pallas_call(
+        body,
+        grid=(steps,),
+        in_specs=[pl.BlockSpec((rows, tile), lambda j: (0, j)), w_spec, whole] + [whole] * len(extra),
+        out_specs=whole,
+        out_shape=jax.ShapeDtypeStruct((rows, width), BF16),
+        scratch_shapes=[pltpu.VMEM((rows, width), F32)],
+        compiler_params=PARAMS,
+        cost_estimate=work(rows, ff, width, 45_000_000),
+    )(value, weights, base, *extra)
+
+
+def back_kernel(layer, cot, w_out, pre):
+    rows, width = cot.shape
+    ff = pre.shape[1]
+    tile, chunk = 512, 256
+
+    def body(g_ref, w_ref, u_ref, v_ref):
+        for first in range(0, rows, chunk):
+            part = pl.ds(first, chunk)
+            v_ref[part, :] = (dot(g_ref[part, :], w_ref[0], NT) * gelu_slope(u_ref[part, :].astype(F32))).astype(BF16)
+
+    return pl.pallas_call(
+        body,
+        grid=(ff // tile,),
+        in_specs=[
+            pl.BlockSpec((rows, width), lambda j: (0, 0)),
+            pl.BlockSpec((1, tile, width), lambda j: (layer, j, 0)),
+            pl.BlockSpec((rows, tile), lambda j: (0, j)),
+        ],
+        out_specs=pl.BlockSpec((rows, tile), lambda j: (0, j)),
+        out_shape=jax.ShapeDtypeStruct((rows, ff), BF16),
+        compiler_params=PARAMS,
+        cost_estimate=work(rows, width, ff, 60_000_000),
+    )(cot, w_out, pre)
+
+
+def gradient_kernel(which, sliced, left, right, theirs, pieces):
+    rows = left[0].shape[0]
+    blk = 1280
+    tile, chunk = 512, 128
+    height = blk // pieces
+    ends = (256, 640, 896, blk)
+    cuts = sorted({0, *ends, *range(0, blk, height)})
+    ranges = [(first, last - first) for first, last in zip(cuts, cuts[1:])]
+    half = rows // tile
+    steps = 2 * half
+
+    def spec(name, far):
+        def index(k, which):
+            row = jnp.maximum(k - half, 0) if far else jnp.minimum(k, half - 1)
+            return row, (which[0] if name == sliced else 0)
+
+        return pl.BlockSpec((tile, blk), index)
+
+    def body(which_ref, lo, lf, ro, rf, *rest):
+        theirs_ref = rest[0] if theirs is not None else None
+        outs = rest[1 if theirs is not None else 0:][:pieces]
+        total, out_sems = rest[-2 - (2 if theirs is not None else 0):][:2]
+        step = pl.program_id(0)
+
+        def product(l_ref, r_ref, first):
+            return dot(l_ref[:, pl.ds(first, chunk)], r_ref[...], TN)
+
+        if theirs is not None:
+            other, other_sem = rest[-2:]
+            fetch = pltpu.make_async_copy(theirs_ref, other, other_sem)
+
+        @pl.when(step == 0)
+        def _():
+            if theirs is not None:
+                fetch.start()
+            for first in range(0, blk, chunk):
+                total[pl.ds(first, chunk), :] = product(lo, ro, first)
+
+        @pl.when(jnp.logical_and(step > 0, step < half))
+        def _():
+            for first in range(0, blk, chunk):
+                total[pl.ds(first, chunk), :] += product(lo, ro, first)
+
+        @pl.when(jnp.logical_and(step >= half, step < steps - 1))
+        def _():
+            for first in range(0, blk, chunk):
+                total[pl.ds(first, chunk), :] += product(lf, rf, first)
+
+        @pl.when(step == steps - 1)
+        def _():
+            if theirs is not None:
+                fetch.wait()
+            copies = []
+            for first in range(0, blk, chunk):
+                part = pl.ds(first, chunk)
+                value = total[part, :] + product(lf, rf, first)
+                total[part, :] = value if theirs is None else value + other[part, :]
+                if first + chunk in ends:
+                    for start, count in ranges[len(copies):]:
+                        if start + count > first + chunk:
+                            break
+                        piece, offset = divmod(start, height)
+                        copies.append(pltpu.make_async_copy(
+                            total.at[pl.ds(start, count), :], outs[piece].at[pl.ds(offset, count), :], out_sems.at[len(copies)]))
+                        copies[-1].start()
+            for copy in copies:
+                copy.wait()
+
+    anywhere = pl.BlockSpec(memory_space=pl.ANY)
+    extra = [] if theirs is None else [theirs]
+    scratch = [pltpu.VMEM((blk, blk), F32), pltpu.SemaphoreType.DMA((len(ranges),))]
+    if theirs is not None:
+        scratch += [pltpu.VMEM((blk, blk), F32), pltpu.SemaphoreType.DMA(())]
+    return pl.pallas_call(
+        body,
+        grid_spec=pltpu.PrefetchScalarGridSpec(
+            num_scalar_prefetch=1,
+            grid=(steps,),
+            in_specs=[spec("left", False), spec("left", True), spec("right", False), spec("right", True)] + [anywhere] * len(extra),
+            out_specs=[anywhere] * pieces,
+            scratch_shapes=scratch,
+        ),
+        out_shape=[jax.ShapeDtypeStruct((blk // pieces, blk), F32)] * pieces,
+        compiler_params=PARAMS,
+        cost_estimate=work(2 * rows, blk, blk, 40_000_000),
+    )(which, *left, *right, *extra)
 
 
 def solution(mesh):
@@ -153,55 +344,38 @@
         scale = 1.0 / math.sqrt(rows * group)
         me = lax.axis_index("data") & 3
         starts = [pl.multiple_of((me ^ flip) * blk, blk) for flip in range(4)]
+        blocks = [jnp.reshape(me ^ flip, (1,)).astype(jnp.int32) for flip in range(2)]
         grads = {"A": blank((layers, ff, width)), "B": blank((layers, width, ff))}
         val = {("o", "h0"): tokens}
 
         def up(side, layer):
-            pre = dot(val[side, f"h{layer}"], w_in[layer], NN).astype(BF16)
-            act = gelu_fn(pre.astype(F32)).astype(BF16)
-            val[side, f"u{layer}"], val[side, f"a{layer}"] = lax.optimization_barrier((pre, act))
+            val[side, f"u{layer}"], val[side, f"a{layer}"] = up_kernel(layer, val[side, f"h{layer}"], w_in)
 
         def down(side, layer):
-            hidden = val[side, f"h{layer}"].astype(F32) + dot(val[side, f"a{layer}"], w_out[layer], NN)
-            hidden = hidden.astype(BF16)
-            if layer < layers - 1:
-                val[side, f"h{layer + 1}"] = hidden
+            last = layer == layers - 1
+            result = down_kernel(layer, val[side, f"a{layer}"], w_out, val[side, f"h{layer}"], NN, targets if last else None, scale)
+            val[side, f"g{layers}" if last else f"h{layer + 1}"] = result
+
+        def back_act(side, layer):
+            val[side, f"v{layer}"] = back_kernel(layer, val[side, f"g{layer + 1}"], w_out, val[side, f"u{layer}"])
+
+        def back_hidden(side, layer):
+            val[side, f"g{layer}"] = down_kernel(layer, val[side, f"v{layer}"], w_in, val[side, f"g{layer + 1}"], NT)
+
+        def partial_sum(name, block):
+            kind, layer = name[0], int(name[1])
+            left, right = ("a", f"g{layer + 1}") if kind == "A" else ("h", f"v{layer}")
+            left = [val[side, f"{left}{layer}"] for side in "of"]
+            right = [val[side, right] for side in "of"]
+            mine = block == "m"
+            parts = gradient_kernel(
+                blocks[0 if mine else 1], "left" if kind == "A" else "right", left, right,
+                val["D", name] if mine else None, PIECES[name] if mine else 1)
+            if mine:
+                for piece, part in enumerate(parts):
+                    val[name, piece] = part
             else:
-                val[side, f"g{layers}"] = ((hidden.astype(F32) - targets.astype(F32)) * scale).astype(BF16)
-
-        def back_act(side, layer):
-            cot, pre = lax.optimization_barrier((val[side, f"g{layer + 1}"], val[side, f"u{layer}"]))
-            d_act = dot(cot, w_out[layer], NT)
-            d_pre = (d_act * gelu_slope(pre.astype(F32))).astype(BF16)
-            val[side, f"v{layer}"] = lax.optimization_barrier(d_pre)
-
-        def back_hidden(side, layer):
-            total = val[side, f"g{layer + 1}"].astype(F32) + dot(val[side, f"v{layer}"], w_in[layer], NT)
-            val[side, f"g{layer}"] = total.astype(BF16)
-
-        def partial_sum(name, block, side):
-            kind, layer = name[0], int(name[1])
-            start = starts[1] if block == "s" else starts[0]
-            if kind == "A":
-                left, right = val[side, f"a{layer}"], val[side, f"g{layer + 1}"]
-                left = lax.dynamic_slice_in_dim(left, start, blk, axis=1)
-            else:
-                left, right = val[side, f"h{layer}"], val[side, f"v{layer}"]
-                right = lax.dynamic_slice_in_dim(right, start, blk, axis=1)
-            total = dot(left, right, TN)
-            if side == "f":
-                total = total + val[name, block]
-                if block == "m":
-                    total = total + val["D", name]
-            else:
-                total = lax.optimization_barrier(total)
-            val[name, block] = val[name, 0] = total
-
-        def split(name):
-            own = val[name, "m"]
-            step = own.shape[0] // PIECES[name]
-            for piece in range(PIECES[name]):
-                val[name, piece] = own[piece * step:(piece + 1) * step]
+                val[name, "s"] = parts[0]
 
         def place(mark, name, piece):
             if mark == "F":
@@ -217,8 +391,6 @@
             mark = item[0]
             if mark in PIECES:
                 partial_sum(*item)
-            elif mark == "S":
-                split(item[1])
             elif mark in PLACES:
                 place(*item)
             else:

time: 3210 us -> 3170 us (0.988)
  matrix products: 1570 us -> 0 us
  Pallas kernels: 0.01 us -> 1390 us
  waiting for transfers between devices: 1280 us -> 1490 us
  local copies, waits for them, and re-layouts: 183 us -> 136 us
    dot_general x59 -> x0, matrix products: 1570 us -> none  [dot(): return lax.dot_general(left, right, dims, preferred_element_type=F32)]
    pallas_call x0 -> x44, Pallas kernels: none -> 1390 us  [the longest x12 442 us: down_kernel(): pl.pallas_call(body, grid=(steps,), in_specs=[pl.BlockSpec((rows, tile),...]
    ppermute x80, waiting for transfers between devices: 1280 us -> 1490 us  [transfer(): val[item] = lax.ppermute(val[source], 'data', route[mark])]
  transfers between devices with their start and end apart: 84 -> 83, of which waited for: 27 -> 30; matrix products, arithmetic and copies ran while one was open for 48% -> 7% of each run, Pallas kernels for 0% -> 35%
where the time goes in v2:
time: 3170 us
  waiting for transfers between devices  1490 us (47%)
  Pallas kernels  1390 us (44%)
  local copies, waits for them, and re-layouts  136 us (4%)
  other arithmetic  74.8 us (2%)
  starting transfers between devices  74.2 us (2%)
    ppermute x80, waiting for transfers between devices, transfer(): val[item] = lax.ppermute(val[source], 'data', route[mark])  1490 us
    pallas_call x12, Pallas kernels, down_kernel(): pl.pallas_call(body, grid=(steps,), in_specs=[pl.BlockSpec((rows, tile),...  442 us
    pallas_call x8, Pallas kernels, back_kernel(): pl.pallas_call(body, grid=(ff // tile,), in_specs=[pl.BlockSpec((rows, wi...  351 us
    pallas_call x16, Pallas kernels, gradient_kernel(): pl.pallas_call(body, grid_spec=pltpu.PrefetchScalarGridSpec(num_scalar_pr...  320 us
    pallas_call x8, Pallas kernels, up_kernel(): pl.pallas_call(body, grid=(ff // tile,), in_specs=[pl.BlockSpec((rows, wi...  281 us
    dynamic_update_slice x54, local copies, waits for them, and re-layouts, place(): grads[kind] = lax.dynamic_update_slice(grads[kind], block[None], where)  134 us
    dynamic_update_slice x18, other arithmetic, place(): grads[kind] = lax.dynamic_update_slice(grads[kind], block[None], where)  74.8 us
    ppermute x80, starting transfers between devices, transfer(): val[item] = lax.ppermute(val[source], 'data', route[mark])  70.7 us
  transfers between devices with their start and end apart: 83, of which 30 were waited for; matrix products, arithmetic and copies ran while one was open for 7% of the time, Pallas kernels for 35%

profile of v2, /device:TPU:1, one launch (start us, length us, event | category | flops | bytes accessed | tf_op | source)
XLA Modules:
  0.0 3165.7 jit_solution(3260895555004776954)
XLA Ops:
  37.9 36.9 %shard_map.61.h_ref.base_ref.lo = bf16[2048,1280]{1,0:T(8,128)(2,1)} custom-call(bf16[2048,5120]{1,0:T(8,128)(2,1)} %get-tuple-element.36.x_ref.lo, bf16[4,5120,1280]{2,1,0:T(8,128)(2,1)} %w_ref.55, bf16[2048,1280]{1,0:T(8,128)(2,1)} %lo.3), custom_call_target="tpu_custom_call" | custom-call | flops 26843545600 | bytes 45000000 | tf_op jit(solution)/shard_map/pallas_call | solution.py:207
  253.0 38.9 %shard_map.69.g_ref.base_ref.ro = bf16[2048,1280]{1,0:T(8,128)(2,1)} custom-call(bf16[2048,5120]{1,0:T(8,128)(2,1)} %get-tuple-element.40.x_ref.lo, bf16[4,5120,1280]{2,1,0:T(8,128)(2,1)} %w_ref.55, bf16[2048,1280]{1,0:T(8,128)(2,1)} %shard_map.65.h_ref.base_ref.lo, bf16[2048,1280]{1,0:T(8,128)(2,1)} %rest_0_.1), custom_call_target="tpu_custom_call" | custom-call | flops 26843545600 | bytes 45000000 | tf_op jit(solution)/shard_map/pallas_call | solution.py:207
  293.4 43.8 %shard_map.70.ro.x_ref = bf16[2048,5120]{1,0:T(8,128)(2,1)} custom-call(bf16[2048,1280]{1,0:T(8,128)(2,1)} %shard_map.69.g_ref.base_ref.ro, bf16[4,5120,1280]{2,1,0:T(8,128)(2,1)} %w_ref.55, bf16[2048,5120]{1,0:T(8,128)(2,1)} %get-tuple-element.41.u_ref), custom_call_target="tpu_custom_call" | custom-call | flops 26843545600 | bytes 60000000 | tf_op jit(solution)/shard_map/pallas_call | solution.py:229
  337.2 37.0 %shard_map.75.g_ref.base_ref.ro = bf16[2048,1280]{1,0:T(8,128)(2,1)} custom-call(bf16[2048,5120]{1,0:T(8,128)(2,1)} %shard_map.70.ro.x_ref, bf16[4,1280,5120]{2,1,0:T(8,128)(2,1)} %w_ref.54, bf16[2048,1280]{1,0:T(8,128)(2,1)} %shard_map.69.g_ref.base_ref.ro), custom_call_target="tpu_custom_call" | custom-call | flops 26843545600 | bytes 45000000 | tf_op jit(solution)/shard_map/pallas_call | solution.py:207
  374.2 43.7 %shard_map.76.ro.x_ref = bf16[2048,5120]{1,0:T(8,128)(2,1)} custom-call(bf16[2048,1280]{1,0:T(8,128)(2,1)} %shard_map.75.g_ref.base_ref.ro, bf16[4,5120,1280]{2,1,0:T(8,128)(2,1)} %w_ref.55, bf16[2048,5120]{1,0:T(8,128)(2,1)} %get-tuple-element.45.u_ref), custom_call_target="tpu_custom_call" | custom-call | flops 26843545600 | bytes 60000000 | tf_op jit(solution)/shard_map/pallas_call | solution.py:229
  454.4 44.0 %shard_map.84.ro.x_ref = bf16[2048,5120]{1,0:T(8,128)(2,1)} custom-call(bf16[2048,1280]{1,0:T(8,128)(2,1)} %shard_map.83.g_ref.base_ref.ro, bf16[4,5120,1280]{2,1,0:T(8,128)(2,1)} %w_ref.55, bf16[2048,5120]{1,0:T(8,128)(2,1)} %get-tuple-element.50.u_ref), custom_call_target="tpu_custom_call" | custom-call | flops 26843545600 | bytes 60000000 | tf_op jit(solution)/shard_map/pallas_call | solution.py:229
  535.0 43.7 %shard_map.91.ro = bf16[2048,5120]{1,0:T(8,128)(2,1)} custom-call(bf16[2048,1280]{1,0:T(8,128)(2,1)} %shard_map.90.g_ref.ro, bf16[4,5120,1280]{2,1,0:T(8,128)(2,1)} %w_ref.55, bf16[2048,5120]{1,0:T(8,128)(2,1)} %get-tuple-element.54.u_ref), custom_call_target="tpu_custom_call" | custom-call | flops 26843545600 | bytes 60000000 | tf_op jit(solution)/shard_map/pallas_call | solution.py:229
  613.9 37.0 %shard_map.82.h_ref.lf = bf16[2048,1280]{1,0:T(8,128)(2,1)} custom-call(bf16[2048,5120]{1,0:T(8,128)(2,1)} %get-tuple-element.49.x_ref.lf, bf16[4,5120,1280]{2,1,0:T(8,128)(2,1)} %w_ref.55, bf16[2048,1280]{1,0:T(8,128)(2,1)} %collective-permute-done.8.h_ref.base_ref.lf), custom_call_target="tpu_custom_call" | custom-call | flops 26843545600 | bytes 45000000 | tf_op jit(solution)/shard_map/pallas_call | solution.py:207
  792.8 43.9 %shard_map.72.rf.x_ref = bf16[2048,5120]{1,0:T(8,128)(2,1)} custom-call(bf16[2048,1280]{1,0:T(8,128)(2,1)} %collective-permute-done.1.g_ref.base_ref.rf, bf16[4,5120,1280]{2,1,0:T(8,128)(2,1)} %w_ref.55, bf16[2048,5120]{1,0:T(8,128)(2,1)} %get-tuple-element.42.u_ref), custom_call_target="tpu_custom_call" | custom-call | flops 26843545600 | bytes 60000000 | tf_op jit(solution)/shard_map/pallas_call | solution.py:229
  912.8 44.1 %shard_map.78.rf.x_ref = bf16[2048,5120]{1,0:T(8,128)(2,1)} custom-call(bf16[2048,1280]{1,0:T(8,128)(2,1)} %shard_map.77.g_ref.base_ref.rf, bf16[4,5120,1280]{2,1,0:T(8,128)(2,1)} %w_ref.55, bf16[2048,5120]{1,0:T(8,128)(2,1)} %get-tuple-element.46.u_ref), custom_call_target="tpu_custom_call" | custom-call | flops 26843545600 | bytes 60000000 | tf_op jit(solution)/shard_map/pallas_call | solution.py:229
  993.6 43.8 %shard_map.87.rf.x_ref = bf16[2048,5120]{1,0:T(8,128)(2,1)} custom-call(bf16[2048,1280]{1,0:T(8,128)(2,1)} %shard_map.85.g_ref.base_ref.rf, bf16[4,5120,1280]{2,1,0:T(8,128)(2,1)} %w_ref.55, bf16[2048,5120]{1,0:T(8,128)(2,1)} %get-tuple-element.51.u_ref), custom_call_target="tpu_custom_call" | custom-call | flops 26843545600 | bytes 60000000 | tf_op jit(solution)/shard_map/pallas_call | solution.py:229
  1115.6 43.7 %shard_map.93.rf = bf16[2048,5120]{1,0:T(8,128)(2,1)} custom-call(bf16[2048,1280]{1,0:T(8,128)(2,1)} %shard_map.92.g_ref.rf, bf16[4,5120,1280]{2,1,0:T(8,128)(2,1)} %w_ref.55, bf16[2048,5120]{1,0:T(8,128)(2,1)} %get-tuple-element.55.u_ref), custom_call_target="tpu_custom_call" | custom-call | flops 26843545600 | bytes 60000000 | tf_op jit(solution)/shard_map/pallas_call | solution.py:229
  1450.1 63.7 %collective-permute-done.51 = f32[640,1280]{1,0:T(8,128)} collective-permute-done((f32[640,1280]{1,0:T(8,128)}, f32[640,1280]{1,0:T(8,128)}, u32[]{:S(2)}, u32[]{:S(2)}) %collective-permute-start.51) | collective-permute-done | bytes 3276832 | tf_op jit(solution)/shard_map/ppermute | solution.py:405
  1519.2 64.8 %collective-permute-done.52 = f32[640,1280]{1,0:T(8,128)} collective-permute-done((f32[640,1280]{1,0:T(8,128)}, f32[640,1280]{1,0:T(8,128)}, u32[]{:S(2)}, u32[]{:S(2)}) %collective-permute-start.52) | collective-permute-done | bytes 3276832 | tf_op jit(solution)/shard_map/ppermute | solution.py:405
  1589.5 64.7 %collective-permute-done.54 = f32[640,1280]{1,0:T(8,128)} collective-permute-done((f32[640,1280]{1,0:T(8,128)}, f32[640,1280]{1,0:T(8,128)}, u32[]{:S(2)}, u32[]{:S(2)}) %collective-permute-start.54) | collective-permute-done | bytes 3276832 | tf_op jit(solution)/shard_map/ppermute | solution.py:405
  1655.5 69.0 %collective-permute-done.55 = f32[640,1280]{1,0:T(8,128)} collective-permute-done((f32[640,1280]{1,0:T(8,128)}, f32[640,1280]{1,0:T(8,128)}, u32[]{:S(2)}, u32[]{:S(2)}) %collective-permute-start.55) | collective-permute-done | bytes 3276832 | tf_op jit(solution)/shard_map/ppermute | solution.py:405
  1734.9 59.7 %collective-permute-done.3 = f32[640,1280]{1,0:T(8,128)} collective-permute-done((f32[640,1280]{1,0:T(8,128)}, f32[640,1280]{1,0:T(8,128)}, u32[]{:S(2)}, u32[]{:S(2)}) %collective-permute-start.3) | collective-permute-done | bytes 3276832 | tf_op jit(solution)/shard_map/ppermute | solution.py:405
  1802.0 62.8 %collective-permute-done.4 = f32[640,1280]{1,0:T(8,128)} collective-permute-done((f32[640,1280]{1,0:T(8,128)S(1)}, f32[640,1280]{1,0:T(8,128)}, u32[]{:S(2)}, u32[]{:S(2)}) %collective-permute-start.4) | collective-permute-done | bytes 3276832 | tf_op jit(solution)/shard_map/ppermute | solution.py:405
  1872.1 63.0 %collective-permute-done.6 = f32[640,1280]{1,0:T(8,128)} collective-permute-done((f32[640,1280]{1,0:T(8,128)S(1)}, f32[640,1280]{1,0:T(8,128)}, u32[]{:S(2)}, u32[]{:S(2)}) %collective-permute-start.6) | collective-permute-done | bytes 3276832 | tf_op jit(solution)/shard_map/ppermute | solution.py:405
  1935.3 70.0 %collective-permute-done.7 = f32[640,1280]{1,0:T(8,128)} collective-permute-done((f32[640,1280]{1,0:T(8,128)S(1)}, f32[640,1280]{1,0:T(8,128)}, u32[]{:S(2)}, u32[]{:S(2)}) %collective-permute-start.7) | collective-permute-done | bytes 3276832 | tf_op jit(solution)/shard_map/ppermute | solution.py:405
  2007.4 68.1 %collective-permute-done.10 = f32[640,1280]{1,0:T(8,128)} collective-permute-done((f32[640,1280]{1,0:T(8,128)S(1)}, f32[640,1280]{1,0:T(8,128)}, u32[]{:S(2)}, u32[]{:S(2)}) %collective-permute-start.10) | collective-permute-done | bytes 3276832 | tf_op jit(solution)/shard_map/ppermute | solution.py:405
  2086.2 59.6 %collective-permute-done.11 = f32[640,1280]{1,0:T(8,128)} collective-permute-done((f32[640,1280]{1,0:T(8,128)S(1)}, f32[640,1280]{1,0:T(8,128)}, u32[]{:S(2)}, u32[]{:S(2)}) %collective-permute-start.11) | collective-permute-done | bytes 3276832 | tf_op jit(solution)/shard_map/ppermute | solution.py:405
  2178.5 48.9 %collective-permute-done.16 = f32[640,1280]{1,0:T(8,128)} collective-permute-done((f32[640,1280]{1,0:T(8,128)S(1)}, f32[640,1280]{1,0:T(8,128)}, u32[]{:S(2)}, u32[]{:S(2)}) %collective-permute-start.16) | collective-permute-done | bytes 3276832 | tf_op jit(solution)/shard_map/ppermute | solution.py:405
  2227.4 70.2 %collective-permute-done.14 = f32[640,1280]{1,0:T(8,128)} collective-permute-done((f32[640,1280]{1,0:T(8,128)}, f32[640,1280]{1,0:T(8,128)}, u32[]{:S(2)}, u32[]{:S(2)}) %collective-permute-start.14) | collective-permute-done | bytes 3276832 | tf_op jit(solution)/shard_map/ppermute | solution.py:405
  2317.9 50.0 %collective-permute-done.20 = f32[640,1280]{1,0:T(8,128)} collective-permute-done((f32[640,1280]{1,0:T(8,128)}, f32[640,1280]{1,0:T(8,128)}, u32[]{:S(2)}, u32[]{:S(2)}) %collective-permute-start.20) | collective-permute-done | bytes 3276832 | tf_op jit(solution)/shard_map/ppermute | solution.py:405
  2390.7 48.3 %collective-permute-done.22 = f32[640,1280]{1,0:T(8,128)S(1)} collective-permute-done((f32[640,1280]{1,0:T(8,128)S(1)}, f32[640,1280]{1,0:T(8,128)S(1)}, u32[]{:S(2)}, u32[]{:S(2)}) %collective-permute-start.22) | collective-permute-done | bytes 3276832 | tf_op jit(solution)/shard_map/ppermute | solution.py:405
  2457.2 52.0 %collective-permute-done.66 = f32[640,1280]{1,0:T(8,128)S(1)} collective-permute-done((f32[640,1280]{1,0:T(8,128)S(1)}, f32[640,1280]{1,0:T(8,128)S(1)}, u32[]{:S(2)}, u32[]{:S(2)}) %collective-permute-start.66) | collective-permute-done | bytes 3276832 | tf_op jit(solution)/shard_map/ppermute | solution.py:405
  2511.1 68.3 %collective-permute-done.26 = f32[640,1280]{1,0:T(8,128)S(1)} collective-permute-done((f32[640,1280]{1,0:T(8,128)S(1)}, f32[640,1280]{1,0:T(8,128)S(1)}, u32[]{:S(2)}, u32[]{:S(2)}) %collective-permute-start.26) | collective-permute-done | bytes 3276832 | tf_op jit(solution)/shard_map/ppermute | solution.py:405
  2596.9 52.7 %collective-permute-done.68 = f32[640,1280]{1,0:T(8,128)S(1)} collective-permute-done((f32[640,1280]{1,0:T(8,128)S(1)}, f32[640,1280]{1,0:T(8,128)S(1)}, u32[]{:S(2)}, u32[]{:S(2)}) %collective-permute-start.68) | collective-permute-done | bytes 3276832 | tf_op jit(solution)/shard_map/ppermute | solution.py:405
  2659.4 60.4 %collective-permute-done.30 = f32[640,1280]{1,0:T(8,128)S(1)} collective-permute-done((f32[640,1280]{1,0:T(8,128)S(1)}, f32[640,1280]{1,0:T(8,128)S(1)}, u32[]{:S(2)}, u32[]{:S(2)}) %collective-permute-start.30) | collective-permute-done | bytes 3276832 | tf_op jit(solution)/shard_map/ppermute | solution.py:405
  2744.2 100.3 %collective-permute-done.33 = f32[320,1280]{1,0:T(8,128)S(1)} collective-permute-done((f32[320,1280]{1,0:T(8,128)S(1)}, f32[320,1280]{1,0:T(8,128)S(1)}, u32[]{:S(2)}, u32[]{:S(2)}) %collective-permute-start.33) | collective-permute-done | bytes 1638432 | tf_op jit(solution)/shard_map/ppermute | solution.py:405
  2979.5 64.7 %collective-permute-done.79 = f32[640,1280]{1,0:T(8,128)S(1)} collective-permute-done((f32[640,1280]{1,0:T(8,128)S(1)}, f32[640,1280]{1,0:T(8,128)S(1)}, u32[]{:S(2)}, u32[]{:S(2)}) %collective-permute-start.79) | collective-permute-done | bytes 3276832 | tf_op jit(solution)/shard_map/ppermute | solution.py:405
  (294 shorter events, 1402.6 us)
Async XLA Ops:
  0.6 578.1 %collective-permute-start.8 = (bf16[2048,1280]{1,0:T(8,128)(2,1)}, bf16[2048,1280]{1,0:T(8,128)(2,1)}, u32[]{:S(2)}, u32[]{:S(2)}) collective-permute-start(bf16[2048,1280]{1,0:T(8,128)(2,1)} %lo.3), channel_id=1, source_target_pairs={{0,2},{1,3},{2,0},{3,1},{4,6},{5,7},{6,4},{7,5}} | collective-permute-start | bytes 15728648 | tf_op jit(solution)/shard_map/ppermute | solution.py:402
  146.2 539.7 %collective-permute-start = (bf16[2048,1280]{1,0:T(8,128)(2,1)}, bf16[2048,1280]{1,0:T(8,128)(2,1)}, u32[]{:S(2)}, u32[]{:S(2)}) collective-permute-start(bf16[2048,1280]{1,0:T(8,128)(2,1)} %shard_map.63.h_ref.base_ref.lo), channel_id=1, source_target_pairs={{0,2},{1,3},{2,0},{3,1},{4,6},{5,7},{6,4},{7,5}} | collective-permute-start | bytes 15728648 | tf_op jit(solution)/shard_map/ppermute | solution.py:402
  291.9 500.8 %collective-permute-start.1 = (bf16[2048,1280]{1,0:T(8,128)(2,1)}, bf16[2048,1280]{1,0:T(8,128)(2,1)}, u32[]{:S(2)}, u32[]{:S(2)}) collective-permute-start(bf16[2048,1280]{1,0:T(8,128)(2,1)} %shard_map.69.g_ref.base_ref.ro), channel_id=1, source_target_pairs={{0,2},{1,3},{2,0},{3,1},{4,6},{5,7},{6,4},{7,5}} | collective-permute-start | bytes 15728648 | tf_op jit(solution)/shard_map/ppermute | solution.py:402
  1095.1 144.9 %collective-permute-start.2 = (f32[1280,1280]{1,0:T(8,128)}, f32[1280,1280]{1,0:T(8,128)}, u32[]{:S(2)}, u32[]{:S(2)}) collective-permute-start(f32[1280,1280]{1,0:T(8,128)} %shard_map.73), channel_id=1, source_target_pairs={{0,1},{1,0},{2,3},{3,2},{4,5},{5,4},{6,7},{7,6}} | collective-permute-start | bytes 19660808 | tf_op jit(solution)/shard_map/ppermute | solution.py:405
  1095.2 165.3 %collective-permute-start.50 = (f32[1280,1280]{1,0:T(8,128)}, f32[1280,1280]{1,0:T(8,128)}, u32[]{:S(2)}, u32[]{:S(2)}) collective-permute-start(f32[1280,1280]{1,0:T(8,128)} %shard_map.99), channel_id=1, source_target_pairs={{0,1},{1,0},{2,3},{3,2},{4,5},{5,4},{6,7},{7,6}} | collective-permute-start | bytes 19660808 | tf_op jit(solution)/shard_map/ppermute | solution.py:405
  1115.5 185.4 %collective-permute-start.5 = (f32[1280,1280]{1,0:T(8,128)}, f32[1280,1280]{1,0:T(8,128)}, u32[]{:S(2)}, u32[]{:S(2)}) collective-permute-start(f32[1280,1280]{1,0:T(8,128)} %shard_map.79), channel_id=1, source_target_pairs={{0,1},{1,0},{2,3},{3,2},{4,5},{5,4},{6,7},{7,6}} | collective-permute-start | bytes 19660808 | tf_op jit(solution)/shard_map/ppermute | solution.py:405
  1342.5 171.3 %collective-permute-start.51 = (f32[640,1280]{1,0:T(8,128)}, f32[640,1280]{1,0:T(8,128)}, u32[]{:S(2)}, u32[]{:S(2)}) collective-permute-start(f32[640,1280]{1,0:T(8,128)} %get-tuple-element.63), channel_id=1, source_target_pairs={{0,4},{1,5},{2,6},{3,7},{4,0},{5,1},{6,2},{7,3}} | collective-permute-start | bytes 9830408 | tf_op jit(solution)/shard_map/ppermute | solution.py:405
  1363.9 220.1 %collective-permute-start.52 = (f32[640,1280]{1,0:T(8,128)}, f32[640,1280]{1,0:T(8,128)}, u32[]{:S(2)}, u32[]{:S(2)}) collective-permute-start(f32[640,1280]{1,0:T(8,128)} %get-tuple-element.64), channel_id=1, source_target_pairs={{0,4},{1,5},{2,6},{3,7},{4,0},{5,1},{6,2},{7,3}} | collective-permute-start | bytes 9830408 | tf_op jit(solution)/shard_map/ppermute | solution.py:405
  1384.1 270.1 %collective-permute-start.54 = (f32[640,1280]{1,0:T(8,128)}, f32[640,1280]{1,0:T(8,128)}, u32[]{:S(2)}, u32[]{:S(2)}) collective-permute-start(f32[640,1280]{1,0:T(8,128)} %get-tuple-element.66), channel_id=1, source_target_pairs={{0,4},{1,5},{2,6},{3,7},{4,0},{5,1},{6,2},{7,3}} | collective-permute-start | bytes 9830408 | tf_op jit(solution)/shard_map/ppermute | solution.py:405
  1405.6 318.8 %collective-permute-start.55 = (f32[640,1280]{1,0:T(8,128)}, f32[640,1280]{1,0:T(8,128)}, u32[]{:S(2)}, u32[]{:S(2)}) collective-permute-start(f32[640,1280]{1,0:T(8,128)} %get-tuple-element.67), channel_id=1, source_target_pairs={{0,4},{1,5},{2,6},{3,7},{4,0},{5,1},{6,2},{7,3}} | collective-permute-start | bytes 9830408 | tf_op jit(solution)/shard_map/ppermute | solution.py:405
  1443.5 351.1 %collective-permute-start.3 = (f32[640,1280]{1,0:T(8,128)}, f32[640,1280]{1,0:T(8,128)}, u32[]{:S(2)}, u32[]{:S(2)}) collective-permute-start(f32[640,1280]{1,0:T(8,128)} %get-tuple-element.43), channel_id=1, source_target_pairs={{0,4},{1,5},{2,6},{3,7},{4,0},{5,1},{6,2},{7,3}} | collective-permute-start | bytes 9830408 | tf_op jit(solution)/shard_map/ppermute | solution.py:405
  1513.8 351.1 %collective-permute-start.4 = (f32[640,1280]{1,0:T(8,128)S(1)}, f32[640,1280]{1,0:T(8,128)}, u32[]{:S(2)}, u32[]{:S(2)}) collective-permute-start(f32[640,1280]{1,0:T(8,128)S(1)} %copy-done.5), channel_id=1, source_target_pairs={{0,4},{1,5},{2,6},{3,7},{4,0},{5,1},{6,2},{7,3}} | collective-permute-start | bytes 9830408 | tf_op jit(solution)/shard_map/ppermute | solution.py:405
  1584.0 351.1 %collective-permute-start.6 = (f32[640,1280]{1,0:T(8,128)S(1)}, f32[640,1280]{1,0:T(8,128)}, u32[]{:S(2)}, u32[]{:S(2)}) collective-permute-start(f32[640,1280]{1,0:T(8,128)S(1)} %copy-done.3), channel_id=1, source_target_pairs={{0,4},{1,5},{2,6},{3,7},{4,0},{5,1},{6,2},{7,3}} | collective-permute-start | bytes 9830408 | tf_op jit(solution)/shard_map/ppermute | solution.py:405
  1654.2 351.1 %collective-permute-start.7 = (f32[640,1280]{1,0:T(8,128)S(1)}, f32[640,1280]{1,0:T(8,128)}, u32[]{:S(2)}, u32[]{:S(2)}) collective-permute-start(f32[640,1280]{1,0:T(8,128)S(1)} %copy-done.2), channel_id=1, source_target_pairs={{0,4},{1,5},{2,6},{3,7},{4,0},{5,1},{6,2},{7,3}} | collective-permute-start | bytes 9830408 | tf_op jit(solution)/shard_map/ppermute | solution.py:405
  1724.4 351.1 %collective-permute-start.10 = (f32[640,1280]{1,0:T(8,128)S(1)}, f32[640,1280]{1,0:T(8,128)}, u32[]{:S(2)}, u32[]{:S(2)}) collective-permute-start(f32[640,1280]{1,0:T(8,128)S(1)} %copy-done.6), channel_id=1, source_target_pairs={{0,4},{1,5},{2,6},{3,7},{4,0},{5,1},{6,2},{7,3}} | collective-permute-start | bytes 9830408 | tf_op jit(solution)/shard_map/ppermute | solution.py:405
  1794.7 351.1 %collective-permute-start.11 = (f32[640,1280]{1,0:T(8,128)S(1)}, f32[640,1280]{1,0:T(8,128)}, u32[]{:S(2)}, u32[]{:S(2)}) collective-permute-start(f32[640,1280]{1,0:T(8,128)S(1)} %copy-done.4), channel_id=1, source_target_pairs={{0,4},{1,5},{2,6},{3,7},{4,0},{5,1},{6,2},{7,3}} | collective-permute-start | bytes 9830408 | tf_op jit(solution)/shard_map/ppermute | solution.py:405
  1864.9 286.3 %collective-permute-start.57 = (f32[640,1280]{1,0:T(8,128)}, f32[640,1280]{1,0:T(8,128)}, u32[]{:S(2)}, u32[]{:S(2)}) collective-permute-start(f32[640,1280]{1,0:T(8,128)} %get-tuple-element.83), channel_id=1, source_target_pairs={{0,1},{1,0},{2,3},{3,2},{4,5},{5,4},{6,7},{7,6}} | collective-permute-start | bytes 9830408 | tf_op jit(solution)/shard_map/ppermute | solution.py:405
  1935.1 220.2 %collective-permute-start.60 = (f32[640,1280]{1,0:T(8,128)}, f32[640,1280]{1,0:T(8,128)}, u32[]{:S(2)}, u32[]{:S(2)}) collective-permute-start(f32[640,1280]{1,0:T(8,128)} %get-tuple-element.83), channel_id=1, source_target_pairs={{0,2},{1,3},{2,0},{3,1},{4,6},{5,7},{6,4},{7,5}} | collective-permute-start | bytes 9830408 | tf_op jit(solution)/shard_map/ppermute | solution.py:405
  2005.3 150.0 %collective-permute-start.56 = (f32[640,1280]{1,0:T(8,128)}, f32[640,1280]{1,0:T(8,128)}, u32[]{:S(2)}, u32[]{:S(2)}) collective-permute-start(f32[640,1280]{1,0:T(8,128)} %get-tuple-element.85), channel_id=1, source_target_pairs={{0,1},{1,0},{2,3},{3,2},{4,5},{5,4},{6,7},{7,6}} | collective-permute-start | bytes 9830408 | tf_op jit(solution)/shard_map/ppermute | solution.py:405
  2155.3 142.3 %collective-permute-start.14 = (f32[640,1280]{1,0:T(8,128)}, f32[640,1280]{1,0:T(8,128)}, u32[]{:S(2)}, u32[]{:S(2)}) collective-permute-start(f32[640,1280]{1,0:T(8,128)} %get-tuple-element.105), channel_id=1, source_target_pairs={{0,2},{1,3},{2,0},{3,1},{4,6},{5,7},{6,4},{7,5}} | collective-permute-start | bytes 9830408 | tf_op jit(solution)/shard_map/ppermute | solution.py:405
  2160.6 143.1 %collective-permute-start.59 = (f32[640,1280]{1,0:T(8,128)}, f32[640,1280]{1,0:T(8,128)S(1)}, u32[]{:S(2)}, u32[]{:S(2)}) collective-permute-start(f32[640,1280]{1,0:T(8,128)} %collective-permute-done.58), channel_id=1, source_target_pairs={{0,1},{1,0},{2,3},{3,2},{4,5},{5,4},{6,7},{7,6}} | collective-permute-start | bytes 9830408 | tf_op jit(solution)/shard_map/ppermute | solution.py:405
  2169.5 140.2 %collective-permute-start.61 = (f32[640,1280]{1,0:T(8,128)}, f32[640,1280]{1,0:T(8,128)S(1)}, u32[]{:S(2)}, u32[]{:S(2)}) collective-permute-start(f32[640,1280]{1,0:T(8,128)} %collective-permute-done.60), channel_id=1, source_target_pairs={{0,1},{1,0},{2,3},{3,2},{4,5},{5,4},{6,7},{7,6}} | collective-permute-start | bytes 9830408 | tf_op jit(solution)/shard_map/ppermute | solution.py:405
  2227.4 140.4 %collective-permute-start.20 = (f32[640,1280]{1,0:T(8,128)}, f32[640,1280]{1,0:T(8,128)}, u32[]{:S(2)}, u32[]{:S(2)}) collective-permute-start(f32[640,1280]{1,0:T(8,128)} %get-tuple-element.101), channel_id=1, source_target_pairs={{0,2},{1,3},{2,0},{3,1},{4,6},{5,7},{6,4},{7,5}} | collective-permute-start | bytes 9830408 | tf_op jit(solution)/shard_map/ppermute | solution.py:405
  2438.9 140.4 %collective-permute-start.26 = (f32[640,1280]{1,0:T(8,128)S(1)}, f32[640,1280]{1,0:T(8,128)S(1)}, u32[]{:S(2)}, u32[]{:S(2)}) collective-permute-start(f32[640,1280]{1,0:T(8,128)S(1)} %get-tuple-element.97), channel_id=1, source_target_pairs={{0,2},{1,3},{2,0},{3,1},{4,6},{5,7},{6,4},{7,5}} | collective-permute-start | bytes 9830408 | tf_op jit(solution)/shard_map/ppermute | solution.py:405
  2442.8 142.8 %collective-permute-start.23 = (f32[640,1280]{1,0:T(8,128)S(1)}, f32[640,1280]{1,0:T(8,128)S(1)}, u32[]{:S(2)}, u32[]{:S(2)}) collective-permute-start(f32[640,1280]{1,0:T(8,128)S(1)} %collective-permute-done.22), channel_id=1, source_target_pairs={{0,1},{1,0},{2,3},{3,2},{4,5},{5,4},{6,7},{7,6}} | collective-permute-start | bytes 9830408 | tf_op jit(solution)/shard_map/ppermute | solution.py:405
  2452.9 138.8 %collective-permute-start.25 = (f32[640,1280]{1,0:T(8,128)S(1)}, f32[640,1280]{1,0:T(8,128)}, u32[]{:S(2)}, u32[]{:S(2)}) collective-permute-start(f32[640,1280]{1,0:T(8,128)S(1)} %get-tuple-element.95), channel_id=1, source_target_pairs={{0,1},{1,0},{2,3},{3,2},{4,5},{5,4},{6,7},{7,6}} | collective-permute-start | bytes 9830408 | tf_op jit(solution)/shard_map/ppermute | solution.py:405
  2509.2 140.4 %collective-permute-start.68 = (f32[640,1280]{1,0:T(8,128)S(1)}, f32[640,1280]{1,0:T(8,128)S(1)}, u32[]{:S(2)}, u32[]{:S(2)}) collective-permute-start(f32[640,1280]{1,0:T(8,128)S(1)} %get-tuple-element.79), channel_id=1, source_target_pairs={{0,2},{1,3},{2,0},{3,1},{4,6},{5,7},{6,4},{7,5}} | collective-permute-start | bytes 9830408 | tf_op jit(solution)/shard_map/ppermute | solution.py:405
  2587.5 139.6 %collective-permute-start.67 = (f32[640,1280]{1,0:T(8,128)S(1)}, f32[640,1280]{1,0:T(8,128)S(1)}, u32[]{:S(2)}, u32[]{:S(2)}) collective-permute-start(f32[640,1280]{1,0:T(8,128)S(1)} %collective-permute-done.66), channel_id=1, source_target_pairs={{0,1},{1,0},{2,3},{3,2},{4,5},{5,4},{6,7},{7,6}} | collective-permute-start | bytes 9830408 | tf_op jit(solution)/shard_map/ppermute | solution.py:405
  2659.4 203.1 %collective-permute-start.73 = (f32[640,1280]{1,0:T(8,128)S(1)}, f32[640,1280]{1,0:T(8,128)S(1)}, u32[]{:S(2)}, u32[]{:S(2)}) collective-permute-start(f32[640,1280]{1,0:T(8,128)S(1)} %get-tuple-element.77), channel_id=1, source_target_pairs={{0,2},{1,3},{2,0},{3,1},{4,6},{5,7},{6,4},{7,5}} | collective-permute-start | bytes 9830408 | tf_op jit(solution)/shard_map/ppermute | solution.py:405
  2953.8 160.5 %collective-permute-start.43 = (f32[320,1280]{1,0:T(8,128)S(1)}, f32[320,1280]{1,0:T(8,128)S(1)}, u32[]{:S(2)}, u32[]{:S(2)}) collective-permute-start(f32[320,1280]{1,0:T(8,128)S(1)} %get-tuple-element.89), channel_id=1, source_target_pairs={{0,2},{1,3},{2,0},{3,1},{4,6},{5,7},{6,4},{7,5}} | collective-permute-start | bytes 4915208 | tf_op jit(solution)/shard_map/ppermute | solution.py:405
  2973.9 142.1 %collective-permute-start.40 = (f32[320,1280]{1,0:T(8,128)S(1)}, f32[320,1280]{1,0:T(8,128)S(1)}, u32[]{:S(2)}, u32[]{:S(2)}) collective-permute-start(f32[320,1280]{1,0:T(8,128)S(1)} %get-tuple-element.87), channel_id=1, source_target_pairs={{0,1},{1,0},{2,3},{3,2},{4,5},{5,4},{6,7},{7,6}} | collective-permute-start | bytes 4915208 | tf_op jit(solution)/shard_map/ppermute | solution.py:405
  2975.6 173.9 %collective-permute-start.45 = (f32[320,1280]{1,0:T(8,128)S(1)}, f32[320,1280]{1,0:T(8,128)S(1)}, u32[]{:S(2)}, u32[]{:S(2)}) collective-permute-start(f32[320,1280]{1,0:T(8,128)S(1)} %get-tuple-element.87), channel_id=1, source_target_pairs={{0,2},{1,3},{2,0},{3,1},{4,6},{5,7},{6,4},{7,5}} | collective-permute-start | bytes 4915208 | tf_op jit(solution)/shard_map/ppermute | solution.py:405
  (72 other events, 5011.2 us)

commit v3 on v2

--- a/solution.py
+++ b/solution.py
@@ -18,33 +18,30 @@
 LAYERS = 4
 SENDS = "XYDEG"
 PLACES = {"F": ("F", 0), "Q": ("X", 2), "R": ("E", 1), "T": ("G", 3)}
-PIECES = {f"{kind}{layer}": 2 for layer in range(LAYERS) for kind in "AB"} | {"B0": 4}
-COST = {"u": 32.0, "d": 32.0, "v": 39.0, "g": 32.0, "grad": 18.0, "sum": 11.0, "place": 7.5,
-        "act": 112.0, "link": 140.0, "core": 13.0, "wake": 2.0, "ahead": 250.0}
-
-
-def sums(name, pieces, after, between):
-    sends = [("Y", name, piece) for piece in range(pieces[name])]
-    return [(name, "s"), ("D", name), *between[:1], (name, "m"), *sends, *between[1:], *after]
+PIECES = {f"{kind}{layer}": 2 for layer in range(LAYERS) for kind in "AB"} | {"A0": 4, "B0": 8}
+COST = {"w": 66.0, "g": 37.0, "u": 35.2, "b": 70.0, "v": 44.0, "grad": 19.8, "sum": 12.2, "place": 7.7, "start": 0.8,
+        "act": 112.0, "link": 140.0, "core": 11.0, "wake": 1.0, "ahead": 1000.0}
+
+
+def core_plan(pieces):
+    def other(name):
+        return [(name, "s"), ("D", name)]
+
+    def mine(name):
+        return [(name, "m"), *(("Y", name, piece) for piece in range(pieces[name]))]
+
+    plan = [("X", "h0"), ("o", "w", 0), ("o", "w", 1), ("X", "h2"), ("o", "w", 2), ("o", "w", 3), ("X", "g4"), ("X", "h1")]
+    plan += [("f", "w", 2), ("f", "u", 3), *other("A3"), *mine("A3")]
+    plan += [("o", "b", 3), ("f", "b", 3), *other("B3"), *other("A2"), *mine("B3")]
+    plan += [("o", "b", 2), *mine("A2"), ("f", "b", 2)]
+    plan += [*other("B2"), ("f", "u", 1), *mine("B2"), *other("A1"), ("o", "b", 1), *mine("A1"), ("f", "b", 1)]
+    plan += [*other("B1"), ("f", "u", 0), *mine("B1"), *other("A0"), ("o", "v", 0), *mine("A0"), ("f", "v", 0)]
+    return plan + [*other("B0"), *mine("B0")]
 
 
 def issue_order(pieces, cost):
-    plan = [("X", "h0")]
-    for layer in range(LAYERS):
-        plan += [("o", "u", layer), ("o", "d", layer)]
-        if layer == 1:
-            plan.append(("X", "h2"))
-    plan.append(("X", f"g{LAYERS}"))
-    plan += [("f", "u", 2), ("f", "d", 2), ("f", "u", 3)]
-    for layer in reversed(range(LAYERS)):
-        one, two = f"A{layer}", f"B{layer}"
-        fill = [("o", "v", layer), ("f", "v", layer)]
-        plan += sums(one, pieces, fill if layer == LAYERS - 1 else [], fill if layer < LAYERS - 1 else [])
-        fill = [("o", "g", layer), ("f", "g", layer)] if layer else []
-        if layer == LAYERS - 2:
-            fill += [("f", "u", 0), ("f", "d", 0), ("f", "u", 1)]
-        plan += sums(two, pieces, [], fill)
-    needs = {("f", "u", 2): ("X", "h2"), ("f", "u", 0): ("X", "h0"), (f"A{LAYERS - 1}", "s"): ("X", f"g{LAYERS}")}
+    plan = core_plan(pieces)
+    needs = {("f", "w", 2): ("X", "h2"), ("f", "u", 1): ("X", "h1"), ("f", "u", 0): ("X", "h0"), ("A3", "s"): ("X", "g4")}
     for name in pieces:
         needs[name, "m"] = ("D", name)
     order, landed, free = [], {}, {"X": 0.0, "Y": 0.0}
@@ -64,7 +61,9 @@
         order.append(item)
 
     def start(item):
+        nonlocal clock
         mark = item[0]
+        clock += cost["start"]
         share = 1 if len(item) == 2 else pieces[item[1]]
         if mark in free:
             length = cost["act"] if item[1] not in pieces else cost["link"] / share
@@ -172,50 +171,6 @@
     )(hidden, w_in)
 
 
-def down_kernel(layer, value, weights, base, dims, target=None, scale=1.0):
-    rows, ff = value.shape
-    width = base.shape[1]
-    tile = 512
-    chunk = 128 if dims == NN else 256
-    steps = ff // tile
-    if dims == NN:
-        w_spec = pl.BlockSpec((1, tile, width), lambda j: (layer, j, 0))
-    else:
-        w_spec = pl.BlockSpec((1, width, tile), lambda j: (layer, 0, j))
-    whole = pl.BlockSpec((rows, width), lambda j: (0, 0))
-
-    def body(x_ref, w_ref, base_ref, *rest):
-        out_ref, total = rest[-2:]
-        step = pl.program_id(0)
-
-        @pl.when(step == 0)
-        def _():
-            total[...] = base_ref[...].astype(F32)
-
-        for first in range(0, rows, chunk):
-            part = pl.ds(first, chunk)
-            total[part, :] += dot(x_ref[part, :], w_ref[0], dims)
-
-        @pl.when(step == steps - 1)
-        def _():
-            result = total[...].astype(BF16)
-            if target is not None:
-                result = ((result.astype(F32) - rest[0][...].astype(F32)) * scale).astype(BF16)
-            out_ref[...] = result
-
-    extra = [] if target is None else [target]
-    return pl.pallas_call(
-        body,
-        grid=(steps,),
-        in_specs=[pl.BlockSpec((rows, tile), lambda j: (0, j)), w_spec, whole] + [whole] * len(extra),
-        out_specs=whole,
-        out_shape=jax.ShapeDtypeStruct((rows, width), BF16),
-        scratch_shapes=[pltpu.VMEM((rows, width), F32)],
-        compiler_params=PARAMS,
-        cost_estimate=work(rows, ff, width, 45_000_000),
-    )(value, weights, base, *extra)
-
-
 def back_kernel(layer, cot, w_out, pre):
     rows, width = cot.shape
     ff = pre.shape[1]
@@ -239,6 +194,104 @@
         compiler_params=PARAMS,
         cost_estimate=work(rows, width, ff, 60_000_000),
     )(cot, w_out, pre)
+
+
+def forward_kernel(layer, hidden, w_in, w_out, target=None, scale=1.0):
+    rows, width = hidden.shape
+    ff = w_in.shape[2]
+    tile, chunk = 512, 128
+    steps = ff // tile
+
+    def body(h_ref, up_ref, down_ref, *rest):
+        u_ref, a_ref, next_ref, total = rest[-4:]
+        step = pl.program_id(0)
+
+        @pl.when(step == 0)
+        def _():
+            total[...] = h_ref[...].astype(F32)
+
+        firsts = list(range(0, rows, chunk))
+        for index in range(len(firsts) + 2):
+            if index < len(firsts):
+                part = pl.ds(firsts[index], chunk)
+                u_ref[part, :] = dot(h_ref[part, :], up_ref[0], NN).astype(BF16)
+            if 1 <= index <= len(firsts):
+                part = pl.ds(firsts[index - 1], chunk)
+                a_ref[part, :] = gelu_fn(u_ref[part, :].astype(F32)).astype(BF16)
+            if index >= 2:
+                part = pl.ds(firsts[index - 2], chunk)
+                total[part, :] += dot(a_ref[part, :], down_ref[0], NN)
+
+        @pl.when(step == steps - 1)
+        def _():
+            result = total[...].astype(BF16)
+            if target is not None:
+                result = ((result.astype(F32) - rest[0][...].astype(F32)) * scale).astype(BF16)
+            next_ref[...] = result
+
+    whole = pl.BlockSpec((rows, width), lambda j: (0, 0))
+    column = pl.BlockSpec((rows, tile), lambda j: (0, j))
+    extra = [] if target is None else [target]
+    return pl.pallas_call(
+        body,
+        grid=(steps,),
+        in_specs=[
+            whole,
+            pl.BlockSpec((1, width, tile), lambda j: (layer, 0, j)),
+            pl.BlockSpec((1, tile, width), lambda j: (layer, j, 0)),
+        ] + [whole] * len(extra),
+        out_specs=[column, column, whole],
+        out_shape=[jax.ShapeDtypeStruct((rows, ff), BF16)] * 2 + [jax.ShapeDtypeStruct((rows, width), BF16)],
+        scratch_shapes=[pltpu.VMEM((rows, width), F32)],
+        compiler_params=PARAMS,
+        cost_estimate=work(rows, width, 2 * ff, 80_000_000),
+    )(hidden, w_in, w_out, *extra)
+
+
+def backward_kernel(layer, cot, w_in, w_out, pre):
+    rows, width = cot.shape
+    ff = pre.shape[1]
+    tile, chunk = 512, 256
+    steps = ff // tile
+
+    def body(g_ref, down_ref, up_ref, u_ref, v_ref, next_ref, total):
+        step = pl.program_id(0)
+
+        @pl.when(step == 0)
+        def _():
+            total[...] = g_ref[...].astype(F32)
+
+        last = None
+        for first in [*range(0, rows, chunk), None]:
+            if first is not None:
+                part = pl.ds(first, chunk)
+                v_ref[part, :] = (dot(g_ref[part, :], down_ref[0], NT) * gelu_slope(u_ref[part, :].astype(F32))).astype(BF16)
+            if last is not None:
+                part = pl.ds(last, chunk)
+                total[part, :] += dot(v_ref[part, :], up_ref[0], NT)
+            last = first
+
+        @pl.when(step == steps - 1)
+        def _():
+            next_ref[...] = total[...].astype(BF16)
+
+    whole = pl.BlockSpec((rows, width), lambda j: (0, 0))
+    column = pl.BlockSpec((rows, tile), lambda j: (0, j))
+    return pl.pallas_call(
+        body,
+        grid=(steps,),
+        in_specs=[
+            whole,
+            pl.BlockSpec((1, tile, width), lambda j: (layer, j, 0)),
+            pl.BlockSpec((1, width, tile), lambda j: (layer, 0, j)),
+            column,
+        ],
+        out_specs=[column, whole],
+        out_shape=[jax.ShapeDtypeStruct((rows, ff), BF16), jax.ShapeDtypeStruct((rows, width), BF16)],
+        scratch_shapes=[pltpu.VMEM((rows, width), F32)],
+        compiler_params=PARAMS,
+        cost_estimate=work(rows, width, 2 * ff, 80_000_000),
+    )(cot, w_out, w_in, pre)
 
 
 def gradient_kernel(which, sliced, left, right, theirs, pieces):
@@ -348,19 +401,21 @@
         grads = {"A": blank((layers, ff, width)), "B": blank((layers, width, ff))}
         val = {("o", "h0"): tokens}
 
+        def forward(side, layer):
+            last = layer == layers - 1
+            pre, act, after = forward_kernel(layer, val[side, f"h{layer}"], w_in, w_out, targets if last else None, scale)
+            val[side, f"u{layer}"], val[side, f"a{layer}"] = pre, act
+            val[side, f"g{layers}" if last else f"h{layer + 1}"] = after
+
         def up(side, layer):
             val[side, f"u{layer}"], val[side, f"a{layer}"] = up_kernel(layer, val[side, f"h{layer}"], w_in)
 
-        def down(side, layer):
-            last = layer == layers - 1
-            result = down_kernel(layer, val[side, f"a{layer}"], w_out, val[side, f"h{layer}"], NN, targets if last else None, scale)
-            val[side, f"g{layers}" if last else f"h{layer + 1}"] = result
+        def backward(side, layer):
+            val[side, f"v{layer}"], val[side, f"g{layer}"] = backward_kernel(
+                layer, val[side, f"g{layer + 1}"], w_in, w_out, val[side, f"u{layer}"])
 
         def back_act(side, layer):
             val[side, f"v{layer}"] = back_kernel(layer, val[side, f"g{layer + 1}"], w_out, val[side, f"u{layer}"])
-
-        def back_hidden(side, layer):
-            val[side, f"g{layer}"] = down_kernel(layer, val[side, f"v{layer}"], w_in, val[side, f"g{layer + 1}"], NT)
 
         def partial_sum(name, block):
             kind, layer = name[0], int(name[1])
@@ -394,7 +449,7 @@
             elif mark in PLACES:
                 place(*item)
             else:
-                {"u": up, "d": down, "v": back_act, "g": back_hidden}[item[1]](mark, item[2])
+                {"w": forward, "u": up, "b": backward, "v": back_act}[item[1]](mark, item[2])
 
         def transfer(item):
             mark, rest = item[0], item[1:]

time: 3170 us -> 3240 us (1.022)
  waiting for transfers between devices: 1490 us -> 1600 us
  Pallas kernels: 1390 us -> 1290 us
  starting transfers between devices: 74.2 us -> 119 us
    pallas_call x12 -> x11, Pallas kernels: 442 us -> 774 us  [the longest x6 434 us: backward_kernel(): pl.pallas_call(body, grid=(steps,), in_specs=[whole, pl.BlockSpec((1, til...]
    pallas_call x8 -> x2, Pallas kernels: 351 us -> 87.6 us  [back_kernel(): pl.pallas_call(body, grid=(ff // tile,), in_specs=[pl.BlockSpec((rows, wi...]
    pallas_call x8 -> x3, Pallas kernels: 281 us -> 105 us  [up_kernel(): pl.pallas_call(body, grid=(ff // tile,), in_specs=[pl.BlockSpec((rows, wi...]
    ppermute x80 -> x104, waiting for transfers between devices: 1490 us -> 1600 us  [transfer(): val[item] = lax.ppermute(val[source], 'data', route[mark])]
    ppermute x80 -> x104, starting transfers between devices: 70.7 us -> 115 us  [transfer(): val[item] = lax.ppermute(val[source], 'data', route[mark])]
    dynamic_update_slice x18 -> x24, other arithmetic: 74.8 us -> 89.5 us  [place(): grads[kind] = lax.dynamic_update_slice(grads[kind], block[None], where)]
    dynamic_update_slice x54 -> x72, local copies, waits for them, and re-layouts: 134 us -> 134 us  [place(): grads[kind] = lax.dynamic_update_slice(grads[kind], block[None], where)]
  transfers between devices with their start and end apart: 83 -> 108, of which waited for: 30 -> 34; matrix products, arithmetic and copies ran while one was open for 7% -> 7% of each run, Pallas kernels for 35% -> 40%
where the time goes in v3:
time: 3240 us; the launch traced here: 3230 us
  waiting for transfers between devices  1600 us (49%)
  Pallas kernels  1290 us (40%)
  local copies, waits for them, and re-layouts  136 us (4%)
  starting transfers between devices  119 us (4%)
  other arithmetic  89.5 us (3%)
    ppermute x104, waiting for transfers between devices, transfer(): val[item] = lax.ppermute(val[source], 'data', route[mark])  1600 us
    pallas_call x6, Pallas kernels, backward_kernel(): pl.pallas_call(body, grid=(steps,), in_specs=[whole, pl.BlockSpec((1, til...  434 us
    pallas_call x5, Pallas kernels, forward_kernel(): pl.pallas_call(body, grid=(steps,), in_specs=[whole, pl.BlockSpec((1, wid...  341 us
    pallas_call x16, Pallas kernels, gradient_kernel(): pl.pallas_call(body, grid_spec=pltpu.PrefetchScalarGridSpec(num_scalar_pr...  321 us
    dynamic_update_slice x72, local copies, waits for them, and re-layouts, place(): grads[kind] = lax.dynamic_update_slice(grads[kind], block[None], where)  134 us
    ppermute x104, starting transfers between devices, transfer(): val[item] = lax.ppermute(val[source], 'data', route[mark])  115 us
    pallas_call x3, Pallas kernels, up_kernel(): pl.pallas_call(body, grid=(ff // tile,), in_specs=[pl.BlockSpec((rows, wi...  105 us
    dynamic_update_slice x24, other arithmetic, place(): grads[kind] = lax.dynamic_update_slice(grads[kind], block[None], where)  89.5 us
  transfers between devices with their start and end apart: 108, of which 34 were waited for; matrix products, arithmetic and copies ran while one was open for 7% of the time, Pallas kernels for 40%

profile of v3, /device:TPU:1, one launch (start us, length us, event | category | flops | bytes accessed | tf_op | source)
XLA Modules:
  0.0 3233.2 jit_solution(8952734918465895834)
XLA Ops:
  2.7 67.3 %shard_map.60 = (bf16[2048,5120]{1,0:T(8,128)(2,1)}, bf16[2048,5120]{1,0:T(8,128)(2,1)}, bf16[2048,1280]{1,0:T(8,128)(2,1)}) custom-call(bf16[2048,1280]{1,0:T(8,128)(2,1)} %lo.3, bf16[4,1280,5120]{2,1,0:T(8,128)(2,1)} %w_ref.8, bf16[4,5120,1280]{2,1,0:T(8,128)(2,1)} %w_ref.9), custom_call_target="tpu_custom_call" | custom-call | flops 53687091200 | bytes 80000000 | tf_op jit(solution)/shard_map/pallas_call | solution.py:235
  70.1 67.6 %shard_map.61 = (bf16[2048,5120]{1,0:T(8,128)(2,1)}, bf16[2048,5120]{1,0:T(8,128)(2,1)}, bf16[2048,1280]{1,0:T(8,128)(2,1)}) custom-call(bf16[2048,1280]{1,0:T(8,128)(2,1)} %get-tuple-element.59.h_ref.lo, bf16[4,1280,5120]{2,1,0:T(8,128)(2,1)} %w_ref.8, bf16[4,5120,1280]{2,1,0:T(8,128)(2,1)} %w_ref.9), custom_call_target="tpu_custom_call" | custom-call | flops 53687091200 | bytes 80000000 | tf_op jit(solution)/shard_map/pallas_call | solution.py:235
  139.2 67.9 %shard_map.62 = (bf16[2048,5120]{1,0:T(8,128)(2,1)}, bf16[2048,5120]{1,0:T(8,128)(2,1)}, bf16[2048,1280]{1,0:T(8,128)(2,1)}) custom-call(bf16[2048,1280]{1,0:T(8,128)(2,1)} %get-tuple-element.60.h_ref.lo, bf16[4,1280,5120]{2,1,0:T(8,128)(2,1)} %w_ref.8, bf16[4,5120,1280]{2,1,0:T(8,128)(2,1)} %w_ref.9), custom_call_target="tpu_custom_call" | custom-call | flops 53687091200 | bytes 80000000 | tf_op jit(solution)/shard_map/pallas_call | solution.py:235
  207.1 70.2 %shard_map.64 = (bf16[2048,5120]{1,0:T(8,128)(2,1)}, bf16[2048,5120]{1,0:T(8,128)(2,1)}, bf16[2048,1280]{1,0:T(8,128)(2,1)}) custom-call(bf16[2048,1280]{1,0:T(8,128)(2,1)} %get-tuple-element.61.h_ref.lo, bf16[4,1280,5120]{2,1,0:T(8,128)(2,1)} %w_ref.8, bf16[4,5120,1280]{2,1,0:T(8,128)(2,1)} %w_ref.9, bf16[2048,1280]{1,0:T(8,128)(2,1)} %rest_0_.1), custom_call_target="tpu_custom_call" | custom-call | flops 53687091200 | bytes 80000000 | tf_op jit(solution)/shard_map/pallas_call | solution.py:235
  277.4 72.3 %shard_map.65 = (bf16[2048,5120]{1,0:T(8,128)(2,1)}, bf16[2048,1280]{1,0:T(8,128)(2,1)}) custom-call(bf16[2048,1280]{1,0:T(8,128)(2,1)} %get-tuple-element.63.g_ref.ro, bf16[4,5120,1280]{2,1,0:T(8,128)(2,1)} %w_ref.9, bf16[4,1280,5120]{2,1,0:T(8,128)(2,1)} %w_ref.8, bf16[2048,5120]{1,0:T(8,128)(2,1)} %get-tuple-element.64.u_ref), custom_call_target="tpu_custom_call" | custom-call | flops 53687091200 | bytes 80000000 | tf_op jit(solution)/shard_map/pallas_call | solution.py:280
  349.6 72.2 %shard_map.70 = (bf16[2048,5120]{1,0:T(8,128)(2,1)}, bf16[2048,1280]{1,0:T(8,128)(2,1)}) custom-call(bf16[2048,1280]{1,0:T(8,128)(2,1)} %get-tuple-element.70.g_ref.ro, bf16[4,5120,1280]{2,1,0:T(8,128)(2,1)} %w_ref.9, bf16[4,1280,5120]{2,1,0:T(8,128)(2,1)} %w_ref.8, bf16[2048,5120]{1,0:T(8,128)(2,1)} %get-tuple-element.71.u_ref), custom_call_target="tpu_custom_call" | custom-call | flops 53687091200 | bytes 80000000 | tf_op jit(solution)/shard_map/pallas_call | solution.py:280
  421.8 72.6 %shard_map.74 = (bf16[2048,5120]{1,0:T(8,128)(2,1)}, bf16[2048,1280]{1,0:T(8,128)(2,1)}) custom-call(bf16[2048,1280]{1,0:T(8,128)(2,1)} %get-tuple-element.78.g_ref.ro, bf16[4,5120,1280]{2,1,0:T(8,128)(2,1)} %w_ref.9, bf16[4,1280,5120]{2,1,0:T(8,128)(2,1)} %w_ref.8, bf16[2048,5120]{1,0:T(8,128)(2,1)} %get-tuple-element.79.u_ref), custom_call_target="tpu_custom_call" | custom-call | flops 53687091200 | bytes 80000000 | tf_op jit(solution)/shard_map/pallas_call | solution.py:280
  538.1 67.5 %shard_map.63 = (bf16[2048,5120]{1,0:T(8,128)(2,1)}, bf16[2048,5120]{1,0:T(8,128)(2,1)}, bf16[2048,1280]{1,0:T(8,128)(2,1)}) custom-call(bf16[2048,1280]{1,0:T(8,128)(2,1)} %collective-permute-done.h_ref.lf, bf16[4,1280,5120]{2,1,0:T(8,128)(2,1)} %w_ref.8, bf16[4,5120,1280]{2,1,0:T(8,128)(2,1)} %w_ref.9), custom_call_target="tpu_custom_call" | custom-call | flops 53687091200 | bytes 80000000 | tf_op jit(solution)/shard_map/pallas_call | solution.py:235
  662.4 72.2 %shard_map.67 = (bf16[2048,5120]{1,0:T(8,128)(2,1)}, bf16[2048,1280]{1,0:T(8,128)(2,1)}) custom-call(bf16[2048,1280]{1,0:T(8,128)(2,1)} %collective-permute-done.1.g_ref.rf, bf16[4,5120,1280]{2,1,0:T(8,128)(2,1)} %w_ref.9, bf16[4,1280,5120]{2,1,0:T(8,128)(2,1)} %w_ref.8, bf16[2048,5120]{1,0:T(8,128)(2,1)} %get-tuple-element.66.u_ref), custom_call_target="tpu_custom_call" | custom-call | flops 53687091200 | bytes 80000000 | tf_op jit(solution)/shard_map/pallas_call | solution.py:280
  775.1 72.2 %shard_map.71 = (bf16[2048,5120]{1,0:T(8,128)(2,1)}, bf16[2048,1280]{1,0:T(8,128)(2,1)}) custom-call(bf16[2048,1280]{1,0:T(8,128)(2,1)} %get-tuple-element.73.g_ref.rf, bf16[4,5120,1280]{2,1,0:T(8,128)(2,1)} %w_ref.9, bf16[4,1280,5120]{2,1,0:T(8,128)(2,1)} %w_ref.8, bf16[2048,5120]{1,0:T(8,128)(2,1)} %get-tuple-element.74.u_ref), custom_call_target="tpu_custom_call" | custom-call | flops 53687091200 | bytes 80000000 | tf_op jit(solution)/shard_map/pallas_call | solution.py:280
  922.8 72.2 %shard_map.76 = (bf16[2048,5120]{1,0:T(8,128)(2,1)}, bf16[2048,1280]{1,0:T(8,128)(2,1)}) custom-call(bf16[2048,1280]{1,0:T(8,128)(2,1)} %get-tuple-element.81.g_ref.rf, bf16[4,5120,1280]{2,1,0:T(8,128)(2,1)} %w_ref.9, bf16[4,1280,5120]{2,1,0:T(8,128)(2,1)} %w_ref.8, bf16[2048,5120]{1,0:T(8,128)(2,1)} %get-tuple-element.82.u_ref), custom_call_target="tpu_custom_call" | custom-call | flops 53687091200 | bytes 80000000 | tf_op jit(solution)/shard_map/pallas_call | solution.py:280
  1344.6 63.9 %collective-permute-done.68 = f32[640,1280]{1,0:T(8,128)} collective-permute-done((f32[640,1280]{1,0:T(8,128)}, f32[640,1280]{1,0:T(8,128)}, u32[]{:S(2)}, u32[]{:S(2)}) %collective-permute-start.68) | collective-permute-done | bytes 3276832 | tf_op jit(solution)/shard_map/ppermute | solution.py:460
  1414.8 63.9 %collective-permute-done.69 = f32[640,1280]{1,0:T(8,128)} collective-permute-done((f32[640,1280]{1,0:T(8,128)}, f32[640,1280]{1,0:T(8,128)}, u32[]{:S(2)}, u32[]{:S(2)}) %collective-permute-start.69) | collective-permute-done | bytes 3276832 | tf_op jit(solution)/shard_map/ppermute | solution.py:460
  1485.0 134.0 %collective-permute-done.71 = f32[640,1280]{1,0:T(8,128)S(1)} collective-permute-done((f32[640,1280]{1,0:T(8,128)}, f32[640,1280]{1,0:T(8,128)S(1)}, u32[]{:S(2)}, u32[]{:S(2)}) %collective-permute-start.71) | collective-permute-done | bytes 3276832 | tf_op jit(solution)/shard_map/ppermute | solution.py:460
  1624.3 65.0 %collective-permute-done.72 = f32[640,1280]{1,0:T(8,128)} collective-permute-done((f32[640,1280]{1,0:T(8,128)}, f32[640,1280]{1,0:T(8,128)}, u32[]{:S(2)}, u32[]{:S(2)}) %collective-permute-start.72) | collective-permute-done | bytes 3276832 | tf_op jit(solution)/shard_map/ppermute | solution.py:460
  1702.0 57.5 %collective-permute-done.4 = f32[640,1280]{1,0:T(8,128)S(1)} collective-permute-done((f32[640,1280]{1,0:T(8,128)}, f32[640,1280]{1,0:T(8,128)S(1)}, u32[]{:S(2)}, u32[]{:S(2)}) %collective-permute-start.4) | collective-permute-done | bytes 3276832 | tf_op jit(solution)/shard_map/ppermute | solution.py:460
  1765.9 63.8 %collective-permute-done.6 = f32[640,1280]{1,0:T(8,128)S(1)} collective-permute-done((f32[640,1280]{1,0:T(8,128)}, f32[640,1280]{1,0:T(8,128)S(1)}, u32[]{:S(2)}, u32[]{:S(2)}) %collective-permute-start.6) | collective-permute-done | bytes 3276832 | tf_op jit(solution)/shard_map/ppermute | solution.py:460
  1833.6 66.4 %collective-permute-done.7 = f32[640,1280]{1,0:T(8,128)} collective-permute-done((f32[640,1280]{1,0:T(8,128)}, f32[640,1280]{1,0:T(8,128)}, u32[]{:S(2)}, u32[]{:S(2)}) %collective-permute-start.7) | collective-permute-done | bytes 3276832 | tf_op jit(solution)/shard_map/ppermute | solution.py:460
  1905.3 64.9 %collective-permute-done.10 = f32[640,1280]{1,0:T(8,128)} collective-permute-done((f32[640,1280]{1,0:T(8,128)}, f32[640,1280]{1,0:T(8,128)}, u32[]{:S(2)}, u32[]{:S(2)}) %collective-permute-start.10) | collective-permute-done | bytes 3276832 | tf_op jit(solution)/shard_map/ppermute | solution.py:460
  1971.5 69.0 %collective-permute-done.11 = f32[640,1280]{1,0:T(8,128)} collective-permute-done((f32[640,1280]{1,0:T(8,128)}, f32[640,1280]{1,0:T(8,128)}, u32[]{:S(2)}, u32[]{:S(2)}) %collective-permute-start.11) | collective-permute-done | bytes 3276832 | tf_op jit(solution)/shard_map/ppermute | solution.py:460
  2134.5 47.7 %collective-permute-done.14 = f32[640,1280]{1,0:T(8,128)S(1)} collective-permute-done((f32[640,1280]{1,0:T(8,128)}, f32[640,1280]{1,0:T(8,128)S(1)}, u32[]{:S(2)}, u32[]{:S(2)}) %collective-permute-start.14) | collective-permute-done | bytes 3276832 | tf_op jit(solution)/shard_map/ppermute | solution.py:460
  2194.9 57.6 %collective-permute-done.80 = f32[640,1280]{1,0:T(8,128)S(1)} collective-permute-done((f32[640,1280]{1,0:T(8,128)S(1)}, f32[640,1280]{1,0:T(8,128)S(1)}, u32[]{:S(2)}, u32[]{:S(2)}) %collective-permute-start.80) | collective-permute-done | bytes 3276832 | tf_op jit(solution)/shard_map/ppermute | solution.py:460
  2266.1 56.5 %collective-permute-done.16 = f32[640,1280]{1,0:T(8,128)S(1)} collective-permute-done((f32[640,1280]{1,0:T(8,128)}, f32[640,1280]{1,0:T(8,128)S(1)}, u32[]{:S(2)}, u32[]{:S(2)}) %collective-permute-start.16) | collective-permute-done | bytes 3276832 | tf_op jit(solution)/shard_map/ppermute | solution.py:460
  2414.5 58.0 %collective-permute-done.23 = f32[640,1280]{1,0:T(8,128)S(1)} collective-permute-done((f32[640,1280]{1,0:T(8,128)S(1)}, f32[640,1280]{1,0:T(8,128)S(1)}, u32[]{:S(2)}, u32[]{:S(2)}) %collective-permute-start.23) | collective-permute-done | bytes 3276832 | tf_op jit(solution)/shard_map/ppermute | solution.py:460
  2479.8 62.9 %collective-permute-done.88 = f32[640,1280]{1,0:T(8,128)S(1)} collective-permute-done((f32[640,1280]{1,0:T(8,128)S(1)}, f32[640,1280]{1,0:T(8,128)S(1)}, u32[]{:S(2)}, u32[]{:S(2)}) %collective-permute-start.88) | collective-permute-done | bytes 3276832 | tf_op jit(solution)/shard_map/ppermute | solution.py:460
  2551.1 61.9 %collective-permute-done.26 = f32[640,1280]{1,0:T(8,128)S(1)} collective-permute-done((f32[640,1280]{1,0:T(8,128)S(1)}, f32[640,1280]{1,0:T(8,128)S(1)}, u32[]{:S(2)}, u32[]{:S(2)}) %collective-permute-start.26) | collective-permute-done | bytes 3276832 | tf_op jit(solution)/shard_map/ppermute | solution.py:460
  2653.6 53.6 %collective-permute-done.33 = f32[640,1280]{1,0:T(8,128)S(1)} collective-permute-done((f32[640,1280]{1,0:T(8,128)S(1)}, f32[640,1280]{1,0:T(8,128)S(1)}, u32[]{:S(2)}, u32[]{:S(2)}) %collective-permute-start.33) | collective-permute-done | bytes 3276832 | tf_op jit(solution)/shard_map/ppermute | solution.py:460
  2713.9 63.5 %collective-permute-done.92 = f32[640,1280]{1,0:T(8,128)S(1)} collective-permute-done((f32[640,1280]{1,0:T(8,128)S(1)}, f32[640,1280]{1,0:T(8,128)S(1)}, u32[]{:S(2)}, u32[]{:S(2)}) %collective-permute-start.92) | collective-permute-done | bytes 3276832 | tf_op jit(solution)/shard_map/ppermute | solution.py:460
  2789.4 58.3 %collective-permute-done.94 = f32[640,1280]{1,0:T(8,128)S(1)} collective-permute-done((f32[640,1280]{1,0:T(8,128)S(1)}, f32[640,1280]{1,0:T(8,128)S(1)}, u32[]{:S(2)}, u32[]{:S(2)}) %collective-permute-start.94) | collective-permute-done | bytes 3276832 | tf_op jit(solution)/shard_map/ppermute | solution.py:460
  2852.7 65.2 %collective-permute-done.36 = f32[640,1280]{1,0:T(8,128)S(1)} collective-permute-done((f32[640,1280]{1,0:T(8,128)S(1)}, f32[640,1280]{1,0:T(8,128)S(1)}, u32[]{:S(2)}, u32[]{:S(2)}) %collective-permute-start.36) | collective-permute-done | bytes 3276832 | tf_op jit(solution)/shard_map/ppermute | solution.py:460
  2946.5 72.9 %collective-permute-done.47 = f32[160,1280]{1,0:T(8,128)S(1)} collective-permute-done((f32[160,1280]{1,0:T(8,128)S(1)}, f32[160,1280]{1,0:T(8,128)S(1)}, u32[]{:S(2)}, u32[]{:S(2)}) %collective-permute-start.47) | collective-permute-done | bytes 819232 | tf_op jit(solution)/shard_map/ppermute | solution.py:460
  3067.3 45.2 %collective-permute-done.54 = f32[160,1280]{1,0:T(8,128)S(1)} collective-permute-done((f32[160,1280]{1,0:T(8,128)S(1)}, f32[160,1280]{1,0:T(8,128)S(1)}, u32[]{:S(2)}, u32[]{:S(2)}) %collective-permute-start.54) | collective-permute-done | bytes 819232 | tf_op jit(solution)/shard_map/ppermute | solution.py:460
  (336 shorter events, 1105.9 us)
Async XLA Ops:
  0.6 994.4 %collective-permute-start.19 = (bf16[2048,1280]{1,0:T(8,128)(2,1)}, bf16[2048,1280]{1,0:T(8,128)(2,1)}, u32[]{:S(2)}, u32[]{:S(2)}) collective-permute-start(bf16[2048,1280]{1,0:T(8,128)(2,1)} %lo.3), channel_id=1, source_target_pairs={{0,2},{1,3},{2,0},{3,1},{4,6},{5,7},{6,4},{7,5}} | collective-permute-start | bytes 15728648 | tf_op jit(solution)/shard_map/ppermute | solution.py:457
  70.0 777.3 %collective-permute-start.8 = (bf16[2048,1280]{1,0:T(8,128)(2,1)}, bf16[2048,1280]{1,0:T(8,128)(2,1)}, u32[]{:S(2)}, u32[]{:S(2)}) collective-permute-start(bf16[2048,1280]{1,0:T(8,128)(2,1)} %get-tuple-element.59.h_ref.lo), channel_id=1, source_target_pairs={{0,2},{1,3},{2,0},{3,1},{4,6},{5,7},{6,4},{7,5}} | collective-permute-start | bytes 15728648 | tf_op jit(solution)/shard_map/ppermute | solution.py:457
  137.7 400.4 %collective-permute-start = (bf16[2048,1280]{1,0:T(8,128)(2,1)}, bf16[2048,1280]{1,0:T(8,128)(2,1)}, u32[]{:S(2)}, u32[]{:S(2)}) collective-permute-start(bf16[2048,1280]{1,0:T(8,128)(2,1)} %get-tuple-element.60.h_ref.lo), channel_id=1, source_target_pairs={{0,2},{1,3},{2,0},{3,1},{4,6},{5,7},{6,4},{7,5}} | collective-permute-start | bytes 15728648 | tf_op jit(solution)/shard_map/ppermute | solution.py:457
  277.2 363.6 %collective-permute-start.1 = (bf16[2048,1280]{1,0:T(8,128)(2,1)}, bf16[2048,1280]{1,0:T(8,128)(2,1)}, u32[]{:S(2)}, u32[]{:S(2)}) collective-permute-start(bf16[2048,1280]{1,0:T(8,128)(2,1)} %get-tuple-element.63.g_ref.ro), channel_id=1, source_target_pairs={{0,2},{1,3},{2,0},{3,1},{4,6},{5,7},{6,4},{7,5}} | collective-permute-start | bytes 15728648 | tf_op jit(solution)/shard_map/ppermute | solution.py:457
  660.8 453.3 %collective-permute-start.64 = (f32[1280,1280]{1,0:T(8,128)}, f32[1280,1280]{1,0:T(8,128)}, u32[]{:S(2)}, u32[]{:S(2)}) collective-permute-start(f32[1280,1280]{1,0:T(8,128)} %shard_map.85), channel_id=1, source_target_pairs={{0,1},{1,0},{2,3},{3,2},{4,5},{5,4},{6,7},{7,6}} | collective-permute-start | bytes 19660808 | tf_op jit(solution)/shard_map/ppermute | solution.py:460
  754.8 379.7 %collective-permute-start.67 = (f32[1280,1280]{1,0:T(8,128)}, f32[1280,1280]{1,0:T(8,128)}, u32[]{:S(2)}, u32[]{:S(2)}) collective-permute-start(f32[1280,1280]{1,0:T(8,128)} %shard_map.87), channel_id=1, source_target_pairs={{0,1},{1,0},{2,3},{3,2},{4,5},{5,4},{6,7},{7,6}} | collective-permute-start | bytes 19660808 | tf_op jit(solution)/shard_map/ppermute | solution.py:460
  774.7 380.4 %collective-permute-start.2 = (f32[1280,1280]{1,0:T(8,128)}, f32[1280,1280]{1,0:T(8,128)}, u32[]{:S(2)}, u32[]{:S(2)}) collective-permute-start(f32[1280,1280]{1,0:T(8,128)} %shard_map.68), channel_id=1, source_target_pairs={{0,1},{1,0},{2,3},{3,2},{4,5},{5,4},{6,7},{7,6}} | collective-permute-start | bytes 19660808 | tf_op jit(solution)/shard_map/ppermute | solution.py:460
  902.5 292.8 %collective-permute-start.70 = (f32[1280,1280]{1,0:T(8,128)}, f32[1280,1280]{1,0:T(8,128)}, u32[]{:S(2)}, u32[]{:S(2)}) collective-permute-start(f32[1280,1280]{1,0:T(8,128)} %shard_map.89), channel_id=1, source_target_pairs={{0,1},{1,0},{2,3},{3,2},{4,5},{5,4},{6,7},{7,6}} | collective-permute-start | bytes 19660808 | tf_op jit(solution)/shard_map/ppermute | solution.py:460
  995.1 222.1 %collective-permute-start.5 = (f32[1280,1280]{1,0:T(8,128)}, f32[1280,1280]{1,0:T(8,128)}, u32[]{:S(2)}, u32[]{:S(2)}) collective-permute-start(f32[1280,1280]{1,0:T(8,128)} %shard_map.72), channel_id=1, source_target_pairs={{0,1},{1,0},{2,3},{3,2},{4,5},{5,4},{6,7},{7,6}} | collective-permute-start | bytes 19660808 | tf_op jit(solution)/shard_map/ppermute | solution.py:460
  1237.2 171.2 %collective-permute-start.68 = (f32[640,1280]{1,0:T(8,128)}, f32[640,1280]{1,0:T(8,128)}, u32[]{:S(2)}, u32[]{:S(2)}) collective-permute-start(f32[640,1280]{1,0:T(8,128)} %get-tuple-element.104), channel_id=1, source_target_pairs={{0,4},{1,5},{2,6},{3,7},{4,0},{5,1},{6,2},{7,3}} | collective-permute-start | bytes 9830408 | tf_op jit(solution)/shard_map/ppermute | solution.py:460
  1258.7 220.0 %collective-permute-start.69 = (f32[640,1280]{1,0:T(8,128)}, f32[640,1280]{1,0:T(8,128)}, u32[]{:S(2)}, u32[]{:S(2)}) collective-permute-start(f32[640,1280]{1,0:T(8,128)} %get-tuple-element.105), channel_id=1, source_target_pairs={{0,4},{1,5},{2,6},{3,7},{4,0},{5,1},{6,2},{7,3}} | collective-permute-start | bytes 9830408 | tf_op jit(solution)/shard_map/ppermute | solution.py:460
  1278.7 416.9 %collective-permute-start.3 = (f32[640,1280]{1,0:T(8,128)}, f32[640,1280]{1,0:T(8,128)}, u32[]{:S(2)}, u32[]{:S(2)}) collective-permute-start(f32[640,1280]{1,0:T(8,128)} %get-tuple-element.68), channel_id=1, source_target_pairs={{0,4},{1,5},{2,6},{3,7},{4,0},{5,1},{6,2},{7,3}} | collective-permute-start | bytes 9830408 | tf_op jit(solution)/shard_map/ppermute | solution.py:460
  1300.7 318.3 %collective-permute-start.71 = (f32[640,1280]{1,0:T(8,128)}, f32[640,1280]{1,0:T(8,128)S(1)}, u32[]{:S(2)}, u32[]{:S(2)}) collective-permute-start(f32[640,1280]{1,0:T(8,128)} %get-tuple-element.108), channel_id=1, source_target_pairs={{0,4},{1,5},{2,6},{3,7},{4,0},{5,1},{6,2},{7,3}} | collective-permute-start | bytes 9830408 | tf_op jit(solution)/shard_map/ppermute | solution.py:460
  1338.2 351.1 %collective-permute-start.72 = (f32[640,1280]{1,0:T(8,128)}, f32[640,1280]{1,0:T(8,128)}, u32[]{:S(2)}, u32[]{:S(2)}) collective-permute-start(f32[640,1280]{1,0:T(8,128)} %get-tuple-element.109), channel_id=1, source_target_pairs={{0,4},{1,5},{2,6},{3,7},{4,0},{5,1},{6,2},{7,3}} | collective-permute-start | bytes 9830408 | tf_op jit(solution)/shard_map/ppermute | solution.py:460
  1408.4 351.0 %collective-permute-start.4 = (f32[640,1280]{1,0:T(8,128)}, f32[640,1280]{1,0:T(8,128)S(1)}, u32[]{:S(2)}, u32[]{:S(2)}) collective-permute-start(f32[640,1280]{1,0:T(8,128)} %get-tuple-element.69), channel_id=1, source_target_pairs={{0,4},{1,5},{2,6},{3,7},{4,0},{5,1},{6,2},{7,3}} | collective-permute-start | bytes 9830408 | tf_op jit(solution)/shard_map/ppermute | solution.py:460
  1478.7 351.0 %collective-permute-start.6 = (f32[640,1280]{1,0:T(8,128)}, f32[640,1280]{1,0:T(8,128)S(1)}, u32[]{:S(2)}, u32[]{:S(2)}) collective-permute-start(f32[640,1280]{1,0:T(8,128)} %get-tuple-element.76), channel_id=1, source_target_pairs={{0,4},{1,5},{2,6},{3,7},{4,0},{5,1},{6,2},{7,3}} | collective-permute-start | bytes 9830408 | tf_op jit(solution)/shard_map/ppermute | solution.py:460
  1619.0 281.0 %collective-permute-start.7 = (f32[640,1280]{1,0:T(8,128)}, f32[640,1280]{1,0:T(8,128)}, u32[]{:S(2)}, u32[]{:S(2)}) collective-permute-start(f32[640,1280]{1,0:T(8,128)} %get-tuple-element.77), channel_id=1, source_target_pairs={{0,4},{1,5},{2,6},{3,7},{4,0},{5,1},{6,2},{7,3}} | collective-permute-start | bytes 9830408 | tf_op jit(solution)/shard_map/ppermute | solution.py:460
  1689.3 280.9 %collective-permute-start.10 = (f32[640,1280]{1,0:T(8,128)}, f32[640,1280]{1,0:T(8,128)}, u32[]{:S(2)}, u32[]{:S(2)}) collective-permute-start(f32[640,1280]{1,0:T(8,128)} %get-tuple-element.84), channel_id=1, source_target_pairs={{0,4},{1,5},{2,6},{3,7},{4,0},{5,1},{6,2},{7,3}} | collective-permute-start | bytes 9830408 | tf_op jit(solution)/shard_map/ppermute | solution.py:460
  1695.7 344.8 %collective-permute-start.11 = (f32[640,1280]{1,0:T(8,128)}, f32[640,1280]{1,0:T(8,128)}, u32[]{:S(2)}, u32[]{:S(2)}) collective-permute-start(f32[640,1280]{1,0:T(8,128)} %get-tuple-element.85), channel_id=1, source_target_pairs={{0,4},{1,5},{2,6},{3,7},{4,0},{5,1},{6,2},{7,3}} | collective-permute-start | bytes 9830408 | tf_op jit(solution)/shard_map/ppermute | solution.py:460
  1759.4 316.1 %collective-permute-start.74 = (f32[320,1280]{1,0:T(8,128)}, f32[320,1280]{1,0:T(8,128)}, u32[]{:S(2)}, u32[]{:S(2)}) collective-permute-start(f32[320,1280]{1,0:T(8,128)} %get-tuple-element.112), channel_id=1, source_target_pairs={{0,4},{1,5},{2,6},{3,7},{4,0},{5,1},{6,2},{7,3}} | collective-permute-start | bytes 4915208 | tf_op jit(solution)/shard_map/ppermute | solution.py:460
  1829.7 286.1 %collective-permute-start.76 = (f32[640,1280]{1,0:T(8,128)}, f32[640,1280]{1,0:T(8,128)}, u32[]{:S(2)}, u32[]{:S(2)}) collective-permute-start(f32[640,1280]{1,0:T(8,128)} %get-tuple-element.135), channel_id=1, source_target_pairs={{0,1},{1,0},{2,3},{3,2},{4,5},{5,4},{6,7},{7,6}} | collective-permute-start | bytes 9830408 | tf_op jit(solution)/shard_map/ppermute | solution.py:460
  1900.0 210.7 %collective-permute-start.75 = (f32[320,1280]{1,0:T(8,128)}, f32[320,1280]{1,0:T(8,128)}, u32[]{:S(2)}, u32[]{:S(2)}) collective-permute-start(f32[320,1280]{1,0:T(8,128)} %get-tuple-element.113), channel_id=1, source_target_pairs={{0,4},{1,5},{2,6},{3,7},{4,0},{5,1},{6,2},{7,3}} | collective-permute-start | bytes 4915208 | tf_op jit(solution)/shard_map/ppermute | solution.py:460
  1970.2 154.8 %collective-permute-start.78 = (f32[640,1280]{1,0:T(8,128)}, f32[640,1280]{1,0:T(8,128)}, u32[]{:S(2)}, u32[]{:S(2)}) collective-permute-start(f32[640,1280]{1,0:T(8,128)} %get-tuple-element.135), channel_id=1, source_target_pairs={{0,2},{1,3},{2,0},{3,1},{4,6},{5,7},{6,4},{7,5}} | collective-permute-start | bytes 9830408 | tf_op jit(solution)/shard_map/ppermute | solution.py:460
  2389.8 153.0 %collective-permute-start.88 = (f32[640,1280]{1,0:T(8,128)S(1)}, f32[640,1280]{1,0:T(8,128)S(1)}, u32[]{:S(2)}, u32[]{:S(2)}) collective-permute-start(f32[640,1280]{1,0:T(8,128)S(1)} %get-tuple-element.129), channel_id=1, source_target_pairs={{0,2},{1,3},{2,0},{3,1},{4,6},{5,7},{6,4},{7,5}} | collective-permute-start | bytes 9830408 | tf_op jit(solution)/shard_map/ppermute | solution.py:460
  2402.3 141.8 %collective-permute-start.87 = (f32[640,1280]{1,0:T(8,128)S(1)}, f32[640,1280]{1,0:T(8,128)S(1)}, u32[]{:S(2)}, u32[]{:S(2)}) collective-permute-start(f32[640,1280]{1,0:T(8,128)S(1)} %collective-permute-done.86), channel_id=1, source_target_pairs={{0,1},{1,0},{2,3},{3,2},{4,5},{5,4},{6,7},{7,6}} | collective-permute-start | bytes 9830408 | tf_op jit(solution)/shard_map/ppermute | solution.py:460
  2413.4 199.6 %collective-permute-start.26 = (f32[640,1280]{1,0:T(8,128)S(1)}, f32[640,1280]{1,0:T(8,128)S(1)}, u32[]{:S(2)}, u32[]{:S(2)}) collective-permute-start(f32[640,1280]{1,0:T(8,128)S(1)} %get-tuple-element.157), channel_id=1, source_target_pairs={{0,2},{1,3},{2,0},{3,1},{4,6},{5,7},{6,4},{7,5}} | collective-permute-start | bytes 9830408 | tf_op jit(solution)/shard_map/ppermute | solution.py:460
  2472.5 141.7 %collective-permute-start.25 = (f32[640,1280]{1,0:T(8,128)S(1)}, f32[640,1280]{1,0:T(8,128)}, u32[]{:S(2)}, u32[]{:S(2)}) collective-permute-start(f32[640,1280]{1,0:T(8,128)S(1)} %collective-permute-done.23), channel_id=1, source_target_pairs={{0,1},{1,0},{2,3},{3,2},{4,5},{5,4},{6,7},{7,6}} | collective-permute-start | bytes 9830408 | tf_op jit(solution)/shard_map/ppermute | solution.py:460
  2652.5 195.2 %collective-permute-start.94 = (f32[640,1280]{1,0:T(8,128)S(1)}, f32[640,1280]{1,0:T(8,128)S(1)}, u32[]{:S(2)}, u32[]{:S(2)}) collective-permute-start(f32[640,1280]{1,0:T(8,128)S(1)} %get-tuple-element.125), channel_id=1, source_target_pairs={{0,2},{1,3},{2,0},{3,1},{4,6},{5,7},{6,4},{7,5}} | collective-permute-start | bytes 9830408 | tf_op jit(solution)/shard_map/ppermute | solution.py:460
  2707.3 141.7 %collective-permute-start.34 = (f32[640,1280]{1,0:T(8,128)S(1)}, f32[640,1280]{1,0:T(8,128)S(1)}, u32[]{:S(2)}, u32[]{:S(2)}) collective-permute-start(f32[640,1280]{1,0:T(8,128)S(1)} %collective-permute-done.33), channel_id=1, source_target_pairs={{0,1},{1,0},{2,3},{3,2},{4,5},{5,4},{6,7},{7,6}} | collective-permute-start | bytes 9830408 | tf_op jit(solution)/shard_map/ppermute | solution.py:460
  2777.5 140.4 %collective-permute-start.36 = (f32[640,1280]{1,0:T(8,128)S(1)}, f32[640,1280]{1,0:T(8,128)S(1)}, u32[]{:S(2)}, u32[]{:S(2)}) collective-permute-start(f32[640,1280]{1,0:T(8,128)S(1)} %get-tuple-element.153), channel_id=1, source_target_pairs={{0,2},{1,3},{2,0},{3,1},{4,6},{5,7},{6,4},{7,5}} | collective-permute-start | bytes 9830408 | tf_op jit(solution)/shard_map/ppermute | solution.py:460
  2778.7 142.2 %collective-permute-start.93 = (f32[640,1280]{1,0:T(8,128)S(1)}, f32[640,1280]{1,0:T(8,128)S(1)}, u32[]{:S(2)}, u32[]{:S(2)}) collective-permute-start(f32[640,1280]{1,0:T(8,128)S(1)} %collective-permute-done.92), channel_id=1, source_target_pairs={{0,1},{1,0},{2,3},{3,2},{4,5},{5,4},{6,7},{7,6}} | collective-permute-start | bytes 9830408 | tf_op jit(solution)/shard_map/ppermute | solution.py:460
  3046.5 142.0 %collective-permute-start.106 = (f32[320,1280]{1,0:T(8,128)S(1)}, f32[320,1280]{1,0:T(8,128)S(1)}, u32[]{:S(2)}, u32[]{:S(2)}) collective-permute-start(f32[320,1280]{1,0:T(8,128)S(1)} %copy-done.2), channel_id=1, source_target_pairs={{0,2},{1,3},{2,0},{3,1},{4,6},{5,7},{6,4},{7,5}} | collective-permute-start | bytes 4915208 | tf_op jit(solution)/shard_map/ppermute | solution.py:460
  (87 other events, 8891.5 us)
